TPU v7x, 128 devices: a whole 4x4x4 slice. The times are simulated.
128 devices in a mesh: dp: 1, ty: 16 (over z, y), tx: 8 (over x, core).
Axes of the slice: x: 4, y: 4, z: 4, core: 2. Of those that a mesh axis runs over, the one named last changes fastest.
Arguments:
- x_in: bfloat16 [3072, 6144], P('dp', 'tx')
- seq_lens: int32 [3072], P('dp')
- k_cache: bfloat16 [3072, 128, 128], P(('dp', 'ty', 'tx'))
- v_cache: bfloat16 [3072, 128, 128], P(('dp', 'ty', 'tx'))
- ln_gamma: float32 [6144], P('tx')
- w_query: bfloat16 [6144, 6144], P('tx', 'ty')
- w_key: bfloat16 [6144, 128], P('tx')
- w_value: bfloat16 [6144, 128], P('tx')
- w_gate: bfloat16 [6144, 24576], P('tx', 'ty')
- w_up: bfloat16 [6144, 24576], P('tx', 'ty')
- w_out: bfloat16 [6144, 6144], P('ty', 'tx')
- w_down: bfloat16 [24576, 6144], P('ty', 'tx')
Outputs:
- output 1: bfloat16 [3072, 6144], P('dp', 'tx')
- output 2: bfloat16 [3072, 128, 128], P(('dp', 'ty', 'tx'))
- output 3: bfloat16 [3072, 128, 128], P(('dp', 'ty', 'tx'))
All inputs are finite; a program needn't handle non-finite values.
Results may differ from a plain program's by a relative error of at most 0.0177021.
Values are sent between devices in bfloat16 or wider.
A program may use at most 1 GiB of HBM per device.

v0:
```python
import jax
import jax.numpy as jnp
from jax import lax
from jax.sharding import PartitionSpec as P

EPSILON = 1e-6
ROPE_BASE = 10000.0


def rope_tables(positions, head_dim):
    half_dim = head_dim // 2
    inv_freqs = ROPE_BASE ** (-(jnp.arange(half_dim, dtype=jnp.float32) * 2.0) / head_dim)
    angles = positions.astype(jnp.float32)[:, None] * inv_freqs[None, :]
    return jnp.cos(angles), jnp.sin(angles)


def rope_apply(vals, cosines, sines):
    half_dim = vals.shape[-1] // 2
    first = vals[..., :half_dim]
    second = vals[..., half_dim:]
    return jnp.concatenate([first * cosines - second * sines, second * cosines + first * sines], axis=-1)


def solution(mesh):
    ty_size = mesh.shape["ty"]
    tx_size = mesh.shape["tx"]
    cache_spec = P(("dp", "ty", "tx"), None, None)

    def layer_shard(x_blk, lens_part, k_blk, v_blk, gamma_blk, w_query, w_key, w_value, w_gate, w_up, w_out, w_down):
        rows = x_blk.shape[0]
        d_model = x_blk.shape[1] * tx_size
        seq_block, ctx_len, head_dim = k_blk.shape
        local_heads = w_query.shape[1] // head_dim
        row_idx = lax.axis_index("ty")
        col_idx = lax.axis_index("tx")

        x_f32 = x_blk.astype(jnp.float32)
        row_stats = jnp.stack([jnp.sum(x_f32, axis=-1), jnp.sum(x_f32 * x_f32, axis=-1)], axis=-1)
        row_stats = lax.psum(row_stats, "tx")
        row_mean = row_stats[:, 0] / d_model
        row_var = row_stats[:, 1] / d_model - row_mean * row_mean
        normed = ((x_f32 - row_mean[:, None]) * lax.rsqrt(row_var[:, None] + EPSILON) * gamma_blk[None, :]).astype(jnp.bfloat16)

        partials = tuple(jnp.dot(normed, weight, preferred_element_type=jnp.float32).astype(jnp.bfloat16) for weight in (w_query, w_key, w_value, w_gate, w_up))
        q_sum, k_sum, v_new, gate, up_proj = lax.psum(partials, "tx")

        cosines, sines = rope_tables(lens_part, head_dim)
        queries = rope_apply(q_sum.astype(jnp.float32).reshape(rows, local_heads, head_dim), cosines[:, None, :], sines[:, None, :]).astype(jnp.bfloat16)
        k_new = rope_apply(k_sum.astype(jnp.float32), cosines, sines).astype(jnp.bfloat16)

        block_start = (row_idx * tx_size + col_idx) * seq_block
        lens_own = lax.dynamic_slice_in_dim(lens_part, block_start, seq_block)
        k_own = lax.dynamic_slice_in_dim(k_new, block_start, seq_block)
        v_own = lax.dynamic_slice_in_dim(v_new, block_start, seq_block)
        positions = jnp.arange(ctx_len)
        at_slot = positions[None, :, None] == lens_own[:, None, None]
        k_out = jnp.where(at_slot, k_own[:, None, :], k_blk)
        v_out = jnp.where(at_slot, v_own[:, None, :], v_blk)

        q_column = lax.dynamic_index_in_dim(queries.reshape(ty_size, tx_size, seq_block, local_heads, head_dim), col_idx, axis=1, keepdims=False)
        q_owned = lax.all_to_all(q_column, "ty", 0, 0, tiled=True)
        scores = jnp.einsum("gbhd,btd->gbht", q_owned, k_out, preferred_element_type=jnp.float32) * (head_dim ** -0.5)
        in_range = positions[None, None, None, :] <= lens_own[None, :, None, None]
        scores = jnp.where(in_range, scores, -1e30)
        att_probs = jax.nn.softmax(scores, axis=-1).astype(jnp.bfloat16)
        att_owned = jnp.einsum("gbht,btd->gbhd", att_probs, v_out, preferred_element_type=jnp.float32).astype(jnp.bfloat16)
        att_column = lax.all_to_all(att_owned, "ty", 0, 0, tiled=True)
        att_rows = lax.all_gather(att_column, "tx", axis=1, tiled=False).reshape(rows, local_heads * head_dim)

        mlp_act = (jax.nn.silu(gate.astype(jnp.float32)) * up_proj.astype(jnp.float32)).astype(jnp.bfloat16)
        part_out = jnp.dot(att_rows, w_out, preferred_element_type=jnp.float32) + jnp.dot(mlp_act, w_down, preferred_element_type=jnp.float32)
        out_sum = lax.psum(part_out.astype(jnp.bfloat16), "ty")
        y_blk = (x_f32 + out_sum.astype(jnp.float32)).astype(jnp.bfloat16)
        return y_blk, k_out, v_out

    in_specs = (P("dp", "tx"), P("dp"), cache_spec, cache_spec, P("tx"), P("tx", "ty"), P("tx", None), P("tx", None), P("tx", "ty"), P("tx", "ty"), P("ty", "tx"), P("ty", "tx"))
    out_specs = (P("dp", "tx"), cache_spec, cache_spec)
    return jax.shard_map(layer_shard, mesh=mesh, in_specs=in_specs, out_specs=out_specs, check_vma=False)
```

profile of v0, /device:TPU:1, one launch (start us, length us, event | category | flops | bytes accessed | tf_op | source)
XLA Modules:
  0.0 518.7 jit_solution(12178290076221151259)
XLA Ops:
  7.2 3.9 convert_reduce_fusion
  11.1 23.6 %psum.49 = f32[3072,2]{0,1:T(2,128)S(1)} all-reduce(f32[3072,2]{0,1:T(2,128)S(1)} %pad_maximum_fusion), channel_id=1, replica_groups=mesh['dp'=1,'ty'=16,'tx'=8] {'tx'}, use_global_device_ids=true, to_apply=%region_2.0 | all-reduce | flops 6144 | bytes 49152 | tf_op jit(solution)/shard_map/psum | solution.py:39
  34.8 3.9 fusion.9
  38.7 9.5 %convolution_convert_fusion = bf16[3072,1536]{1,0:T(8,128)(2,1)} fusion(bf16[3072,768]{1,0:T(8,128)(2,1)S(1)} %fusion.9, bf16[768,1536]{1,0:T(8,128)(2,1)S(1)} %copy-done), kind=kOutput, calls=%fused_computation.12 | convolution fusion | flops 7252475904 | bytes 16515072 | tf_op jit(solution)/shard_map/dot_general | solution.py:44
  48.3 9.6 %convolution_convert_fusion.1 = bf16[3072,1536]{1,0:T(8,128)(2,1)} fusion(bf16[3072,768]{1,0:T(8,128)(2,1)S(1)} %fusion.9, bf16[768,1536]{1,0:T(8,128)(2,1)S(1)} %copy-done.11), kind=kOutput, calls=%fused_computation.13 | convolution fusion | flops 7252475904 | bytes 16515072 | tf_op jit(solution)/shard_map/dot_general | solution.py:44
  57.8 2.1 convolution_convert_fusion.2
  60.0 2.5 copy.34
  62.5 4.8 convolution_convert_fusion.3
  67.2 2.3 convolution_convert_fusion.4
  70.4 241.3 %all-reduce.6.cloned.1.call-done = (bf16[3072,1536]{1,0:T(8,128)(2,1)}, bf16[3072,1536]{1,0:T(8,128)(2,1)}, bf16[3072,128]{1,0:T(8,128)(2,1)}, bf16[3072,128]{1,0:T(8,128)(2,1)}, bf16[3072,3,128]{2,0,1:T(8,128)(2,1)}) async-done(((bf16[3072,1536]{1,0:T(8,128)(2,1)}, bf16[3072,1536]{1,0:T(8,128)(2,1)}, bf16[3072,128]{1,0:T(8,128)(2,1)}, bf16[3072,128]{1,0:T(8,128)(2,1)}, bf16[3072,3,128]{2,0,1:T(8,128)(2,1)}), ...) | async-done | bytes 22806544 | tf_op jit(solution)/shard_map/psum | solution.py:45
  312.9 2.0 reshape.126
  314.9 7.5 %multiply_cosine_fusion = (f32[3072,64]{1,0:T(8,128)S(1)}, f32[3072,64]{1,0:T(8,128)S(1)}, bf16[3072,64]{1,0:T(8,128)(2,1)S(1)}, bf16[3072,64]{1,0:T(8,128)(2,1)}) fusion(f32[64]{0:T(128)S(1)} %multiply_power_fusion, f32[3072]{0:T(1024)S(1)} %convert_element_type.63, f32[3072,128]{1,0:T(8,128)S(1)} %convert_element_type.62), kind=kLoop, calls=%fused_computation.29 | loop fusion | flops 1769472 | bytes 3944704 | tf_op jit(solution)/shard_map/cos | solution.py:14
  322.4 1.7 add_convert_fusion.1
  325.0 6.7 %all-to-all-start = ((bf16[16,24,3,128]{3,1,2,0:T(8,128)(2,1)}), bf16[16,24,3,128]{3,1,2,0:T(8,128)(2,1)S(1)}, u32[]{:S(2)}, u32[]{:S(2)}) async-start(bf16[16,24,3,128]{3,1,2,0:T(8,128)(2,1)} %copy_bitcast_fusion), calls=%async_computation | async-start | bytes 589824 | tf_op jit(solution)/shard_map/all_to_all | solution.py:61
  334.4 4.7 all-to-all-done
  340.3 2.0 fusion.17
  342.4 11.4 %all_to_all.10 = bf16[16,24,3,128]{3,1,2,0:T(8,128)(2,1)S(1)} all-to-all(bf16[16,24,3,128]{3,1,2,0:T(8,128)(2,1)S(1)} %copy.37), channel_id=1, replica_groups=mesh['dp'=1,'ty'=16,'tx'=8] {'ty'}, dimensions={0} | all-to-all | bytes 589824 | tf_op jit(solution)/shard_map/all_to_all | solution.py:67
  354.6 18.0 %fusion.11 = f32[3072,768]{1,0:T(8,128)} fusion(bf16[1536,768]{1,0:T(8,128)(2,1)} %param.23, bf16[3072,1536]{1,0:T(8,128)(2,1)} %get-tuple-element.5, bf16[3072,1536]{1,0:T(8,128)(2,1)} %get-tuple-element.6), kind=kOutput, calls=%fused_computation.20 | convolution fusion | flops 7285506048 | bytes 30670848 | tf_op jit(solution)/shard_map/dot_general | solution.py:71
  372.6 7.3 %all-gather.3.cloned.1.call-done = bf16[16,192,3,128]{3,0,2,1:T(8,128)(2,1)} async-done(((bf16[16,24,3,128]{3,0,2,1:T(8,128)(2,1)}), bf16[16,192,3,128]{3,0,2,1:T(8,128)(2,1)}) %all-gather.3.cloned.1.call-update) | async-done | bytes 2359312 | tf_op jit(solution)/shard_map/all_gather | solution.py:68
  379.9 5.4 %copy.39 = bf16[16,192,3,128]{1,0,3,2:T(8,128)(2,1)} copy(bf16[16,192,3,128]{3,0,2,1:T(8,128)(2,1)} %all-gather.3.cloned.1.call-done) | data formatting | bytes 4718592 | tf_op jit(solution)/shard_map/all_gather | solution.py:68
  385.3 5.1 reshape.127
  390.4 6.6 %add_convert_fusion = bf16[3072,768]{1,0:T(8,128)(2,1)} fusion(f32[3072,768]{1,0:T(8,128)} %fusion.11, bf16[3072,384]{0,1:T(8,128)(2,1)S(1)} %reshape.127, bf16[384,768]{1,0:T(8,128)(2,1)S(1)} %copy-done.6), kind=kOutput, calls=%fused_computation.19 | convolution fusion | flops 1816657920 | bytes 17104896 | tf_op jit(solution)/shard_map/dot_general | solution.py:71
  397.0 108.0 %all-reduce.4.cloned.1.call-done = bf16[3072,768]{1,0:T(8,128)(2,1)} async-done(((bf16[3072,768]{1,0:T(8,128)(2,1)}), bf16[3072,768]{1,0:T(8,128)(2,1)}) %all-reduce.4.cloned.1.call-update) | async-done | bytes 4718608 | tf_op jit(solution)/shard_map/psum | solution.py:72
  505.1 7.2 %fusion.10 = bf16[3072,768]{1,0:T(8,128)(2,1)} fusion(bf16[3072,768]{1,0:T(8,128)(2,1)} %param.12, bf16[3072,768]{1,0:T(8,128)(2,1)} %all-reduce.4.cloned.1.call-done), kind=kLoop, calls=%fused_computation.18 | loop fusion | flops 9437184 | bytes 14155776 | tf_op jit(solution)/shard_map/convert_element_type | solution.py:73
  (46 shorter events, 7.8 us)
Async XLA Ops:
  7.2 31.5 %copy-start = (bf16[768,1536]{1,0:T(8,128)(2,1)S(1)}, bf16[768,1536]{1,0:T(8,128)(2,1)}, u32[]{:S(2)}) copy-start(bf16[768,1536]{1,0:T(8,128)(2,1)} %param.21) | copy-start | bytes 7077892
  7.2 27.6 %copy-start.10 = (f32[768]{0:T(1024)S(1)}, f32[768]{0:T(1024)}, u32[]{:S(2)}) copy-start(f32[768]{0:T(1024)} %param.16) | copy-start | bytes 9220
  7.2 304.5 %all-reduce.6.cloned.1.call-start = ((), (), s32[]{:S(2)}) async-start(), calls=%async_computation.4 | async-start | bytes 45613056 | tf_op jit(solution)/shard_map/psum | solution.py:45
  38.7 19.1 %copy-start.2 = (bf16[3072,768]{1,0:T(8,128)(2,1)}, bf16[3072,768]{1,0:T(8,128)(2,1)S(1)}, u32[]{:S(2)}) copy-start(bf16[3072,768]{1,0:T(8,128)(2,1)S(1)} %fusion.9) | copy-start | bytes 14155780
  38.7 9.6 %copy-start.11 = (bf16[768,1536]{1,0:T(8,128)(2,1)S(1)}, bf16[768,1536]{1,0:T(8,128)(2,1)}, u32[]{:S(2)}) copy-start(bf16[768,1536]{1,0:T(8,128)(2,1)} %param.20) | copy-start | bytes 7077892
  48.3 9.6 %copy-start.12 = (bf16[768,384]{1,0:T(8,128)(2,1)S(1)}, bf16[768,384]{1,0:T(8,128)(2,1)}, u32[]{:S(2)}) copy-start(bf16[768,384]{1,0:T(8,128)(2,1)} %param.17) | copy-start | bytes 1769476
  60.0 2.5 copy-start.7
  62.5 4.8 copy-start.3
  62.5 4.8 copy-start.8
  69.5 0.7 copy-start.9
  325.0 14.2 %all-to-all-start = ((bf16[16,24,3,128]{3,1,2,0:T(8,128)(2,1)}), bf16[16,24,3,128]{3,1,2,0:T(8,128)(2,1)S(1)}, u32[]{:S(2)}, u32[]{:S(2)}) async-start(bf16[16,24,3,128]{3,1,2,0:T(8,128)(2,1)} %copy_bitcast_fusion), calls=%async_computation | async-start | bytes 589824 | tf_op jit(solution)/shard_map/all_to_all | solution.py:61
  331.7 48.2 %all-gather.3.cloned.1.call-start = ((), (), s32[]{:S(2)}) async-start(), calls=%async_computation.3 | async-start | bytes 2654208 | tf_op jit(solution)/shard_map/all_gather | solution.py:68
  334.4 38.2 %copy-start.4 = (bf16[24,128,128]{2,1,0:T(8,128)(2,1)}, bf16[24,128,128]{2,1,0:T(8,128)(2,1)S(1)}, u32[]{:S(2)}) copy-start(bf16[24,128,128]{2,1,0:T(8,128)(2,1)S(1)} %get-tuple-element.20) | copy-start | bytes 2359300
  334.4 38.2 %copy-start.5 = (bf16[24,128,128]{2,1,0:T(8,128)(2,1)}, bf16[24,128,128]{2,1,0:T(8,128)(2,1)S(1)}, u32[]{:S(2)}) copy-start(bf16[24,128,128]{2,1,0:T(8,128)(2,1)S(1)} %get-tuple-element.21) | copy-start | bytes 2359300
  354.6 150.5 %all-reduce.4.cloned.1.call-start = ((), (), s32[]{:S(2)}) async-start(), calls=%async_computation.2 | async-start | bytes 9437184 | tf_op jit(solution)/shard_map/psum | solution.py:72
  379.9 10.5 %copy-start.6 = (bf16[384,768]{1,0:T(8,128)(2,1)S(1)}, bf16[384,768]{1,0:T(8,128)(2,1)}, u32[]{:S(2)}) copy-start(bf16[384,768]{1,0:T(8,128)(2,1)} %param.22) | copy-start | bytes 1769476
  397.0 115.2 %copy-start.1 = (bf16[768,1536]{1,0:T(8,128)(2,1)S(1)}, bf16[768,1536]{1,0:T(8,128)(2,1)}, u32[]{:S(2)}) copy-start(bf16[768,1536]{1,0:T(8,128)(2,1)} %param.21) | copy-start | bytes 7077892
Sparse Core Ops, SparseCore 0:
  69.7 241.9 all-reduce.5
  354.7 25.1 all-gather.2
  397.1 107.8 all-reduce.3
where the time goes:
time: 519 us
  waiting for transfers between devices  361 us (70%)
  matrix products  55.6 us (11%)
  blocking collectives  35 us (7%)
  other arithmetic  31.3 us (6%)
  local copies, waits for them, and re-layouts  14.6 us (3%)
  between operations  13.9 us (3%)
  starting transfers between devices  7 us (1%)
    psum x1, waiting for transfers between devices, layer_shard(): q_sum, k_sum, v_new, gate, up_proj = lax.psum(partials, 'tx')  241 us
    psum x1, waiting for transfers between devices, layer_shard(): out_sum = lax.psum(part_out.astype(jnp.bfloat16), 'ty')  108 us
    dot_general x5, matrix products, layer_shard(): jnp.dot(normed, weight, preferred_element_type=jnp.float32)  28.3 us
    psum x1, blocking collectives, layer_shard(): row_stats = lax.psum(row_stats, 'tx')  23.6 us
    dot_general x1, matrix products, layer_shard(): jnp.dot(mlp_act, w_down, preferred_element_type=jnp.float32)  18 us
    all_to_all x1, blocking collectives, layer_shard(): att_column = lax.all_to_all(att_owned, 'ty', 0, 0, tiled=True)  11.4 us
  transfers between devices with their start and end apart: 4, of which 4 were waited for; matrix products, arithmetic and copies ran while one was open for 4% of the time, Pallas kernels for 0%

commit v1 on v0

v1 whole, which is shorter than its diff:
```python
import functools

import jax
import jax.numpy as jnp
from jax import lax
from jax.experimental import pallas as pl
from jax.experimental.pallas import tpu as pltpu
from jax.sharding import PartitionSpec as P

EPSILON = 1e-6
ROPE_BASE = 10000.0
MESH = pl.DeviceIdType.MESH
RING = 4
F32 = jnp.float32
BF16 = jnp.bfloat16


def rope_tables(positions, head_dim):
    half_dim = head_dim // 2
    inv_freqs = ROPE_BASE ** (-(jnp.arange(half_dim, dtype=F32) * 2.0) / head_dim)
    angles = positions.astype(F32)[:, None] * inv_freqs[None, :]
    cosines, sines = jnp.cos(angles), jnp.sin(angles)
    return jnp.concatenate([cosines, cosines], axis=-1), jnp.concatenate([-sines, sines], axis=-1)


def remote(src, dst, send_sem, recv_sem, ty, tx):
    return pltpu.make_async_remote_copy(
        src_ref=src, dst_ref=dst, send_sem=send_sem, recv_sem=recv_sem,
        device_id={"ty": ty, "tx": tx}, device_id_type=MESH,
    )


def project_kernel(
    ty_size, tile, d_model,
    x_main, x_kv, wq, wkv, wg, wu, gamma, cos_q, sin_q, cos_kv, sin_kv,
    act_out, q_out, kv_out,
    xs, ws, wkvs, gam, st, sr, p2, sd, sb, ra, rb, act, kvs, kvr, kvf, qs, qr,
    load_sem, pair_send, pair_recv, st_send, st_recv, ssem, rsem, kv_ssem, kv_rsem, kvf_sem, q_ssem, q_rsem, out_sem,
):
    row_idx = lax.axis_index("ty")
    col_idx = lax.axis_index("tx")
    ring_pos, core = col_idx // 2, col_idx % 2
    other = 1 - core
    half_ty = ty_size // 2
    group = xs.shape[1]
    seq_block = group // 2
    rows = half_ty * group
    hrows = rows // 2
    hg = half_ty // 2
    kdim = xs.shape[2]
    kblk = kdim // 2
    steps = wg.shape[1] // tile
    head_dim = cos_q.shape[1]
    q_width = wq.shape[1]
    pos_p, pos_m, pos_o = (ring_pos + 1) % RING, (ring_pos + RING - 1) % RING, (ring_pos + 2) % RING
    tx_p, tx_m, tx_o = pos_p * 2 + core, pos_m * 2 + core, pos_o * 2 + core
    tx_pair = ring_pos * 2 + other
    lanes = pl.ds(pl.multiple_of(core * kblk, 128), kblk)
    krows = pl.ds(pl.multiple_of(core * kblk, 128), kblk)

    pieces = []
    for d in range(RING):
        pieces.append((lambda c, d=d: x_main.at[c, :, d], xs.at[pl.ds(d * half_ty, half_ty), :, lanes]))
    pieces.append((lambda c: x_kv.at[row_idx], xs.at[pl.ds(RING * half_ty, RING), :, lanes]))
    pieces.append((lambda c: gamma, gam.at[:, lanes]))
    pieces.append((lambda c: wq, ws.at[0, krows, pl.ds(0, q_width)]))
    pieces.append((lambda c: wkv.at[c], wkvs.at[krows]))
    for t in range(steps):
        pieces.append((lambda c, t=t: wg.at[:, pl.ds(t * tile, tile)], ws.at[t + 1, krows, pl.ds(0, tile)]))
        pieces.append((lambda c, t=t: wu.at[:, pl.ds(t * tile, tile)], ws.at[t + 1, krows, pl.ds(tile, tile)]))
    loads = [pltpu.make_async_copy(src(core), dst, load_sem.at[n]) for n, (src, dst) in enumerate(pieces)]
    swaps = [remote(src(other), dst, pair_send.at[n], pair_recv.at[n], row_idx, tx_pair) for n, (src, dst) in enumerate(pieces)]
    for load in loads:
        load.start()
    st[...] = jnp.zeros_like(st)

    barrier = pltpu.get_barrier_semaphore()
    pl.semaphore_signal(barrier, inc=1, device_id={"ty": row_idx, "tx": tx_pair}, device_id_type=MESH)
    for tx in (tx_p, tx_m, tx_o):
        pl.semaphore_signal(barrier, inc=1, device_id={"ty": row_idx, "tx": tx}, device_id_type=MESH)
    for off in range(1, ty_size):
        for cc in range(2):
            pl.semaphore_signal(
                barrier, inc=1, device_id={"ty": (row_idx + off) % ty_size, "tx": ring_pos * 2 + cc}, device_id_type=MESH
            )
    pl.semaphore_wait(barrier, 4 + 2 * (ty_size - 1))
    for swap in swaps:
        swap.start()
    for n in range(6):
        loads[n].wait()
        swaps[n].wait_recv()

    blk = 2 * group
    blocks = (RING * half_ty + RING) // 2
    lane_tiles = kdim // 128

    def stat_block(b, _):
        def lane_tile(j, sums):
            part = xs[pl.ds(2 * b, 2), :, pl.ds(pl.multiple_of(j * 128, 128), 128)].reshape(blk, 128).astype(F32)
            return sums[0] + part, sums[1] + part * part
        zero = jnp.zeros((blk, 128), F32)
        s1, s2 = lax.fori_loop(0, lane_tiles, lane_tile, (zero, zero))
        st[pl.ds(b, 1), pl.ds(0, blk)] = jnp.sum(s1.T, axis=0, keepdims=True)
        st[pl.ds(b + st.shape[0] // 2, 1), pl.ds(0, blk)] = jnp.sum(s2.T, axis=0, keepdims=True)
        return 0

    lax.fori_loop(0, blocks, stat_block, 0)
    stat_copies = [
        remote(st, sr.at[n], st_send.at[n], st_recv.at[n], row_idx, tx) for n, tx in enumerate((tx_p, tx_m, tx_o))
    ]
    for copy in stat_copies:
        copy.start()
    for copy in stat_copies:
        copy.wait()
    total = ((st[...] + sr[0]) + (sr[1] + sr[2]))
    mean = total[: st.shape[0] // 2] / d_model
    var = total[st.shape[0] // 2 :] / d_model - mean * mean
    sr[0, : st.shape[0] // 2, :] = mean
    sr[1, : st.shape[0] // 2, :] = lax.rsqrt(var + EPSILON)

    def norm_block(b, _):
        mean_b = jnp.broadcast_to(sr[0, pl.ds(b, 1), :], (128, 128)).T[:blk]
        rstd_b = jnp.broadcast_to(sr[1, pl.ds(b, 1), :], (128, 128)).T[:blk]
        for j in range(lane_tiles):
            cols = slice(j * 128, (j + 1) * 128)
            part = xs[pl.ds(2 * b, 2), :, cols].reshape(blk, 128).astype(F32)
            normed = ((part - mean_b) * rstd_b * gam[0:1, cols]).astype(BF16)
            xs[pl.ds(2 * b, 2), :, cols] = normed.reshape(2, group, 128)
        return 0

    lax.fori_loop(0, blocks, norm_block, 0)

    def left(start, count):
        return xs[pl.ds(start, count)].reshape(count * group, kdim)

    def mm(start, count, w):
        return jnp.dot(left(start, count), w, preferred_element_type=F32)

    def hop(s, n, kind, side):
        cols = pl.ds(0, n)
        src, dst = (
            (p2.at[s, pl.ds(side * hrows, hrows), cols], ra.at[s, side, :, cols]),
            (sd.at[s, side, :, cols], rb.at[s, side, 0, :, cols]),
            (sb.at[s, side, :, cols], rb.at[s, side, 1, :, cols]),
        )[kind]
        return remote(src, dst, ssem.at[s, kind, side], rsem.at[s, kind, side], row_idx, (tx_p, tx_m)[side])

    def stage_a(s, n):
        w = ws[s, :, 0:n]
        p2[s, :, 0:n] = mm(pos_o * half_ty, half_ty, w).astype(BF16)
        hop(s, n, 0, 0).start()
        hop(s, n, 0, 1).start()
        sd[s, 0, :, 0:n] = mm(pos_p * half_ty + hg, hg, w).astype(BF16)
        hop(s, n, 1, 0).start()
        sd[s, 1, :, 0:n] = mm(pos_m * half_ty, hg, w).astype(BF16)
        hop(s, n, 1, 1).start()

    def stage_b(s, n):
        w = ws[s, :, 0:n]
        for side, start in ((0, pos_p * half_ty), (1, pos_m * half_ty + hg)):
            own = mm(start, hg, w)
            hop(s, n, 0, side).wait_recv()
            sb[s, side, :, 0:n] = (own + ra[s, side, :, 0:n].astype(F32)).astype(BF16)
            hop(s, n, 2, side).start()

    def stage_c(s, n, finish):
        w = ws[s, :, 0:n]
        for half in range(2):
            own = mm(ring_pos * half_ty + half * hg, hg, w)
            hop(s, n, 2, half).wait_recv()
            hop(s, n, 1, 1 - half).wait_recv()
            finish(half, own + rb[s, half, 1, :, 0:n].astype(F32) + rb[s, 1 - half, 0, :, 0:n].astype(F32))

    def turn(vals, cos2, sin2):
        return vals * cos2 + pltpu.roll(vals, head_dim // 2, 1) * sin2

    def finish_q(half, vals):
        tab = pl.ds(half * hrows, hrows)
        for h in range(q_width // head_dim):
            cols = slice(h * head_dim, (h + 1) * head_dim)
            turned = turn(vals[:, cols], cos_q[tab, :], sin_q[tab, :])
            for k in range(2 * hg):
                qs[half * 2 * hg + k, :, cols] = turned[k * seq_block : (k + 1) * seq_block].astype(BF16)

    def finish_mlp(s):
        def finish(half, vals):
            gate = vals[:, :tile].astype(BF16).astype(F32)
            up = vals[:, tile:].astype(BF16).astype(F32)
            act[pl.ds(half * hrows, hrows), pl.ds(pl.multiple_of((s - 1) * tile, tile), tile)] = (
                gate * jax.nn.sigmoid(gate) * up
            ).astype(BF16)
        return finish

    def q_copy(k):
        return remote(
            qs.at[k], qr.at[row_idx], q_ssem.at[k], q_rsem.at[row_idx],
            core * half_ty + k // 2, ring_pos * 2 + k % 2,
        )

    def q_is_self(k):
        return jnp.logical_and(core * half_ty + k // 2 == row_idx, core == k % 2)

    def kv_copy(n, pos):
        return remote(kvs.at[pos], kvr.at[n], kv_ssem.at[n], kv_rsem.at[n], row_idx, pos * 2 + core)

    wide = 2 * tile
    loads[6].wait()
    swaps[6].wait_recv()
    stage_a(0, q_width)
    loads[7].wait()
    swaps[7].wait_recv()
    kvs[...] = mm(RING * half_ty, RING, wkvs[...]).reshape(kvs.shape)
    for n, pos in enumerate((pos_p, pos_m, pos_o)):
        kv_copy(n, pos).start()
    for n in range(8, len(loads)):
        loads[n].wait()
        swaps[n].wait_recv()
    stage_a(1, wide)
    stage_b(0, q_width)
    for n, pos in enumerate((pos_p, pos_m, pos_o)):
        kv_copy(n, pos).wait_recv()
    new_row = (kvs[ring_pos] + kvr[0]) + (kvr[1] + kvr[2])
    kvf[core] = turn(new_row, cos_kv[...], sin_kv[...]).astype(BF16)
    kv_pair = remote(kvf.at[core], kvf.at[core], kvf_sem.at[0], kvf_sem.at[1], row_idx, tx_pair)
    kv_pair.start()
    stage_a(2, wide)
    stage_b(1, wide)
    stage_c(0, q_width, finish_q)
    for k in range(ty_size):
        @pl.when(q_is_self(k))
        def _():
            pltpu.make_async_copy(qs.at[k], qr.at[row_idx], q_rsem.at[row_idx]).start()

        @pl.when(jnp.logical_not(q_is_self(k)))
        def _():
            q_copy(k).start()

    def middle(s, _):
        stage_a(s, wide)
        stage_b(s - 1, wide)
        stage_c(s - 2, wide, finish_mlp(s - 2))
        return 0

    lax.fori_loop(3, steps + 1, middle, 0)
    stage_b(steps, wide)
    stage_c(steps - 1, wide, finish_mlp(steps - 1))
    stage_c(steps, wide, finish_mlp(steps))

    outs = [
        pltpu.make_async_copy(act, act_out, out_sem.at[0]),
        pltpu.make_async_copy(qr, q_out, out_sem.at[1]),
        pltpu.make_async_copy(kvf, kv_out, out_sem.at[2]),
    ]
    outs[0].start()
    for k in range(ty_size):
        remote(qs.at[0], qr.at[k], q_ssem.at[0], q_rsem.at[k], row_idx, tx_pair).wait_recv()
    outs[1].start()
    kv_pair.wait_send()
    remote(kvf.at[other], kvf.at[other], kvf_sem.at[0], kvf_sem.at[1], row_idx, tx_pair).wait_recv()
    outs[2].start()
    for k in range(ty_size):
        @pl.when(jnp.logical_not(q_is_self(k)))
        def _():
            q_copy(k).wait_send()
    for n, pos in enumerate((pos_p, pos_m, pos_o)):
        kv_copy(n, pos).wait_send()
    for swap in swaps:
        swap.wait_send()
    for kind in range(3):
        for side in range(2):
            hop(0, q_width, kind, side).wait_send()

    def drain(s, _):
        for kind in range(3):
            for side in range(2):
                hop(s, wide, kind, side).wait_send()
        return 0

    lax.fori_loop(1, steps + 1, drain, 0)
    for out in outs:
        out.wait()


def project(x_blk, gamma_blk, wq, wk, wv, wg, wu, cos_q, sin_q, cos_kv, sin_kv, ty_size, seq_block, d_model, tile):
    rows_all, kblk = x_blk.shape
    half_ty, group = ty_size // 2, 2 * seq_block
    rows = half_ty * group
    q_width, ffn = wq.shape[1], wg.shape[1]
    kv_width = wk.shape[1]
    steps = ffn // tile
    wide = 2 * tile
    kdim = 2 * kblk
    x_main = x_blk.reshape(2, half_ty, RING, group, kblk)
    x_kv = x_blk.reshape(ty_size, RING, group, kblk)
    wkv = jnp.stack([wk, wv])
    gamma = jnp.broadcast_to(gamma_blk[None, :], (8, kblk))
    pieces = RING + 4 + 2 * steps
    stat_lines = 2 * (-(-((RING * half_ty + RING) // 2) // 8) * 8)
    any_spec = pl.BlockSpec(memory_space=pl.ANY)
    vmem_spec = pl.BlockSpec(memory_space=pltpu.VMEM)
    return pl.pallas_call(
        functools.partial(project_kernel, ty_size, tile, d_model),
        out_shape=(
            jax.ShapeDtypeStruct((rows, ffn), BF16),
            jax.ShapeDtypeStruct((ty_size, seq_block, q_width), BF16),
            jax.ShapeDtypeStruct((2, group, kv_width), BF16),
        ),
        in_specs=[any_spec] * 7 + [vmem_spec] * 4,
        out_specs=(any_spec,) * 3,
        scratch_shapes=[
            pltpu.VMEM((RING * half_ty + RING, group, kdim), BF16),
            pltpu.VMEM((steps + 1, kdim, wide), BF16),
            pltpu.VMEM((kdim, kv_width), BF16),
            pltpu.VMEM((8, kdim), F32),
            pltpu.VMEM((stat_lines, 128), F32),
            pltpu.VMEM((3, stat_lines, 128), F32),
            pltpu.VMEM((steps + 1, rows, wide), BF16),
            pltpu.VMEM((steps + 1, 2, rows // 2, wide), BF16),
            pltpu.VMEM((steps + 1, 2, rows // 2, wide), BF16),
            pltpu.VMEM((steps + 1, 2, rows // 2, wide), BF16),
            pltpu.VMEM((steps + 1, 2, 2, rows // 2, wide), BF16),
            pltpu.VMEM((rows, ffn), BF16),
            pltpu.VMEM((RING, group, kv_width), F32),
            pltpu.VMEM((3, group, kv_width), F32),
            pltpu.VMEM((2, group, kv_width), BF16),
            pltpu.VMEM((ty_size, seq_block, q_width), BF16),
            pltpu.VMEM((ty_size, seq_block, q_width), BF16),
            pltpu.SemaphoreType.DMA((pieces,)),
            pltpu.SemaphoreType.DMA((pieces,)),
            pltpu.SemaphoreType.DMA((pieces,)),
            pltpu.SemaphoreType.DMA((3,)),
            pltpu.SemaphoreType.DMA((3,)),
            pltpu.SemaphoreType.DMA((steps + 1, 3, 2)),
            pltpu.SemaphoreType.DMA((steps + 1, 3, 2)),
            pltpu.SemaphoreType.DMA((3,)),
            pltpu.SemaphoreType.DMA((3,)),
            pltpu.SemaphoreType.DMA((2,)),
            pltpu.SemaphoreType.DMA((ty_size,)),
            pltpu.SemaphoreType.DMA((ty_size,)),
            pltpu.SemaphoreType.DMA((3,)),
        ],
        compiler_params=pltpu.CompilerParams(
            collective_id=0, has_side_effects=True, vmem_limit_bytes=56 * 1024 * 1024
        ),
        name="project",
    )(x_main, x_kv, wq, wkv, wg, wu, gamma, cos_q, sin_q, cos_kv, sin_kv)


def solution(mesh):
    ty_size = mesh.shape["ty"]
    tx_size = mesh.shape["tx"]
    cache_spec = P(("dp", "ty", "tx"), None, None)

    def layer_shard(x_blk, lens_part, k_blk, v_blk, gamma_blk, w_query, w_key, w_value, w_gate, w_up, w_out, w_down):
        rows = x_blk.shape[0]
        d_model = x_blk.shape[1] * tx_size
        seq_block, ctx_len, head_dim = k_blk.shape
        half_ty, group = ty_size // 2, 2 * seq_block
        local_heads = w_query.shape[1] // head_dim
        row_idx = lax.axis_index("ty")
        col_idx = lax.axis_index("tx")
        ring_pos, core = col_idx // 2, col_idx % 2
        tile = min(256, w_gate.shape[1])

        lens_q = lax.dynamic_slice(lens_part.reshape(2, half_ty, RING, group), (core, 0, ring_pos, 0), (1, half_ty, 1, group))
        cos_q, sin_q = rope_tables(lens_q.reshape(-1), head_dim)
        block_start = (row_idx * tx_size + col_idx) * seq_block
        lens_own = lax.dynamic_slice_in_dim(lens_part, block_start, seq_block)
        lens_kv = lax.dynamic_slice_in_dim(lens_part, (row_idx * RING + ring_pos) * group, group)
        cos_kv, sin_kv = rope_tables(jnp.where(core == 0, lens_kv, 0), head_dim)

        act_own, q_owned, kv_new = project(
            x_blk, gamma_blk, w_query, w_key, w_value, w_gate, w_up, cos_q, sin_q, cos_kv, sin_kv,
            ty_size, seq_block, d_model, tile,
        )
        kv_own = lax.dynamic_slice_in_dim(kv_new, core * seq_block, seq_block, axis=1)
        positions = jnp.arange(ctx_len)
        at_slot = positions[None, :, None] == lens_own[:, None, None]
        k_out = jnp.where(at_slot, kv_own[0][:, None, :], k_blk)
        v_out = jnp.where(at_slot, kv_own[1][:, None, :], v_blk)

        q_owned = q_owned.reshape(ty_size, seq_block, local_heads, head_dim)
        scores = jnp.einsum("gbhd,btd->gbht", q_owned, k_out, preferred_element_type=F32) * (head_dim ** -0.5)
        in_range = positions[None, None, None, :] <= lens_own[None, :, None, None]
        scores = jnp.where(in_range, scores, -1e30)
        att_probs = jax.nn.softmax(scores, axis=-1).astype(BF16)
        att_owned = jnp.einsum("gbht,btd->gbhd", att_probs, v_out, preferred_element_type=F32).astype(BF16)
        att_column = lax.all_to_all(att_owned, "ty", 0, 0, tiled=True)
        att_rows = lax.all_gather(att_column, "tx", axis=1, tiled=False).reshape(rows, local_heads * head_dim)

        mlp_all = lax.all_gather(act_own, "tx", axis=0, tiled=False)
        mlp_act = mlp_all.reshape(RING, 2, half_ty, group, -1).transpose(1, 2, 0, 3, 4).reshape(rows, -1)
        part_out = jnp.dot(att_rows, w_out, preferred_element_type=F32) + jnp.dot(mlp_act, w_down, preferred_element_type=F32)
        out_sum = lax.psum(part_out.astype(BF16), "ty")
        y_blk = (x_blk.astype(F32) + out_sum.astype(F32)).astype(BF16)
        return y_blk, k_out, v_out

    in_specs = (P("dp", "tx"), P("dp"), cache_spec, cache_spec, P("tx"), P("tx", "ty"), P("tx", None), P("tx", None), P("tx", "ty"), P("tx", "ty"), P("ty", "tx"), P("ty", "tx"))
    out_specs = (P("dp", "tx"), cache_spec, cache_spec)
    return jax.shard_map(layer_shard, mesh=mesh, in_specs=in_specs, out_specs=out_specs, check_vma=False)
```

time: 519 us -> 382 us (0.74)
  waiting for transfers between devices: 361 us -> 176 us
  Pallas kernels: 0 us -> 118 us
  matrix products: 55.6 us -> 19.2 us
  blocking collectives: 35 us -> 11.4 us
  other arithmetic: 31.3 us -> 15.2 us
  local copies, waits for them, and re-layouts: 14.6 us -> 26.5 us
  starting transfers between devices: 7 us -> 0.34 us
    psum x2 -> x1, waiting for transfers between devices: 349 us -> 108 us  [layer_shard(): out_sum = lax.psum(part_out.astype(BF16), 'ty')]
    pallas_call x0 -> x1, Pallas kernels: none -> 118 us  [project(): pl.pallas_call(functools.partial(project_kernel, ty_size, tile, d_model),...]
    all_gather x0 -> x1, waiting for transfers between devices: none -> 44.6 us  [layer_shard(): mlp_all = lax.all_gather(act_own, 'tx', axis=0, tiled=False)]
    dot_general x9 -> x4, matrix products: 55.6 us -> 19.2 us  [the longest x1 10.5 us: layer_shard(): jnp.dot(mlp_act, w_down, preferred_element_type=F32)]
    psum x1 -> x0, blocking collectives: 23.6 us -> none  [layer_shard(): row_stats = lax.psum(row_stats, 'tx')]
    all_gather x1, waiting for transfers between devices: 7.27 us -> 23 us  [layer_shard(): lax.all_gather(att_column, 'tx', axis=1, tiled=False)]
    reshape x1 -> x3, local copies, waits for them, and re-layouts: 2.49 us -> 10.5 us  [the longest x1 8.21 us: layer_shard(): mlp_all.reshape(RING, 2, half_ty, group, -1).transpose(1, 2, 0, 3, 4)]
    cos x1 -> x0, other arithmetic: 7.48 us -> none  [rope_tables(): return (jnp.cos(angles), jnp.sin(angles))]
  transfers between devices with their start and end apart: 4 -> 3, of which waited for: 4 -> 3; matrix products, arithmetic and copies ran while one was open for 4% -> 3% of each run, Pallas kernels for 0% -> 0%
where the time goes in v1:
time: 382 us; the launch traced here: 381 us
  waiting for transfers between devices  176 us (46%)
  Pallas kernels  118 us (31%)
  local copies, waits for them, and re-layouts  26.5 us (7%)
  matrix products  19.2 us (5%)
  other arithmetic  15.2 us (4%)
  between operations  13.9 us (4%)
  blocking collectives  11.4 us (3%)
    pallas_call x1, Pallas kernels, project(): pl.pallas_call(functools.partial(project_kernel, ty_size, tile, d_model),...  118 us
    psum x1, waiting for transfers between devices, layer_shard(): out_sum = lax.psum(part_out.astype(BF16), 'ty')  108 us
    all_gather x1, waiting for transfers between devices, layer_shard(): mlp_all = lax.all_gather(act_own, 'tx', axis=0, tiled=False)  44.6 us
    all_gather x1, waiting for transfers between devices, layer_shard(): lax.all_gather(att_column, 'tx', axis=1, tiled=False)  23 us
    all_to_all x1, blocking collectives, layer_shard(): att_column = lax.all_to_all(att_owned, 'ty', 0, 0, tiled=True)  11.4 us
    dot_general x1, matrix products, layer_shard(): jnp.dot(mlp_act, w_down, preferred_element_type=F32)  10.5 us
    reshape x1, local copies, waits for them, and re-layouts, layer_shard(): mlp_all.reshape(RING, 2, half_ty, group, -1).transpose(1, 2, 0, 3, 4)  8.21 us
  transfers between devices with their start and end apart: 3, of which 3 were waited for; matrix products, arithmetic and copies ran while one was open for 3% of the time, Pallas kernels for 0%

profile of v1, /device:TPU:1, one launch (start us, length us, event | category | flops | bytes accessed | tf_op | source)
XLA Modules:
  0.0 380.9 jit_solution(15038501890070213811)
XLA Ops:
  7.3 0.9 reshape.96
  8.2 0.8 dynamic_slice.12
  9.2 0.8 fusion.12
  10.1 0.8 fusion.10
  10.9 1.8 pad_maximum_fusion.wkv
  13.4 0.9 pad_maximum_fusion.1
  14.3 1.3 broadcast_in_dim.61.gamma
  15.6 118.1 %project.1 = (bf16[384,1536]{1,0:T(8,128)(2,1)}, bf16[16,24,384]{2,1,0:T(8,128)(2,1)}, bf16[2,48,128]{2,1,0:T(8,128)(2,1)}) custom-call(bf16[2,8,4,48,768]{4,3,2,1,0:T(8,128)(2,1)} %bitcast.36, bf16[16,4,48,768]{3,2,1,0:T(8,128)(2,1)} %bitcast.37, bf16[768,384]{1,0:T(8,128)(2,1)} %wq.1, bf16[2,768,128]{2,1,0:T(8,128)(2,1)} %pad_maximum_fusion.wkv, ...), custom_call_target="tpu_custom_call" | custom-call | tf_op jit(solution)/shard_map/project/pallas_call | solution.py:301
  133.8 1.3 reshape.97
  135.1 0.7 dynamic-slice_bitcast_fusion
  135.8 2.4 broadcast_select_fusion
  138.9 0.8 copy-done.4
  140.1 3.6 fusion.5
  143.9 11.4 %all_to_all.5 = bf16[16,24,3,128]{3,1,2,0:T(8,128)(2,1)S(1)} all-to-all(bf16[16,24,3,128]{3,1,2,0:T(8,128)(2,1)S(1)} %copy.25), channel_id=1, replica_groups=mesh['dp'=1,'ty'=16,'tx'=8] {'ty'}, dimensions={0} | all-to-all | bytes 589824 | tf_op jit(solution)/shard_map/all_to_all | solution.py:388
  155.2 0.8 copy.26
  157.0 23.0 %all-gather.5.cloned.1.call-done = bf16[16,192,3,128]{3,0,2,1:T(8,128)(2,1)} async-done(((bf16[16,24,3,128]{3,0,2,1:T(8,128)(2,1)}), bf16[16,192,3,128]{3,0,2,1:T(8,128)(2,1)}) %all-gather.5.cloned.1.call-update) | async-done | bytes 2359312 | tf_op jit(solution)/shard_map/all_gather | solution.py:389
  180.0 5.3 %copy.27 = bf16[16,192,3,128]{1,0,3,2:T(8,128)(2,1)} copy(bf16[16,192,3,128]{3,0,2,1:T(8,128)(2,1)} %all-gather.5.cloned.1.call-done) | data formatting | bytes 4718592 | tf_op jit(solution)/shard_map/all_gather | solution.py:389
  185.4 6.2 %reshape.98 = bf16[3072,384]{0,1:T(8,128)(2,1)} reshape(bf16[16,192,3,128]{1,0,3,2:T(8,128)(2,1)} %copy.27) | data formatting | bytes 4718592 | tf_op jit(solution)/shard_map/reshape | solution.py:389
  191.5 44.6 %all-gather.7.cloned.1.call-done = bf16[3072,1536]{1,0:T(8,128)(2,1)} async-done(((bf16[384,1536]{1,0:T(8,128)(2,1)}), bf16[3072,1536]{1,0:T(8,128)(2,1)}) %all-gather.7.cloned.1.call-update) | async-done | bytes 9437200 | tf_op jit(solution)/shard_map/all_gather | solution.py:391
  236.1 8.2 %copy.28 = bf16[4,2,8,48,1536]{4,3,0,2,1:T(8,128)(2,1)} copy(bf16[4,2,8,48,1536]{4,3,2,1,0:T(8,128)(2,1)} %bitcast.38) | data formatting | bytes 18874368 | tf_op jit(solution)/shard_map/reshape | solution.py:392
  244.4 10.5 %fusion.15 = f32[3072,768]{1,0:T(8,128)S(1)} fusion(bf16[3072,1536]{1,0:T(8,128)(2,1)} %bitcast.39, bf16[1536,768]{1,0:T(8,128)(2,1)S(1)} %copy-done), kind=kOutput, calls=%fused_computation.38 | convolution fusion | flops 7247757312 | bytes 21233664 | tf_op jit(solution)/shard_map/dot_general | solution.py:393
  254.9 4.5 %add_convert_fusion.1 = bf16[3072,768]{1,0:T(8,128)(2,1)} fusion(f32[3072,768]{1,0:T(8,128)S(1)} %fusion.15, bf16[3072,384]{0,1:T(8,128)(2,1)S(1)} %copy-done.2, bf16[384,768]{1,0:T(8,128)(2,1)S(1)} %copy-done.5), kind=kOutput, calls=%fused_computation.2 | convolution fusion | flops 1816657920 | bytes 17104896 | tf_op jit(solution)/shard_map/dot_general | solution.py:393
  259.4 107.9 %all-reduce.2.cloned.1.call-done = bf16[3072,768]{1,0:T(8,128)(2,1)} async-done(((bf16[3072,768]{1,0:T(8,128)(2,1)}), bf16[3072,768]{1,0:T(8,128)(2,1)}) %all-reduce.2.cloned.1.call-update) | async-done | bytes 4718608 | tf_op jit(solution)/shard_map/psum | solution.py:394
  367.2 7.2 %add_convert_fusion = bf16[3072,768]{1,0:T(8,128)(2,1)} fusion(bf16[3072,768]{1,0:T(8,128)(2,1)} %all-reduce.2.cloned.1.call-done, bf16[3072,768]{1,0:T(8,128)(2,1)} %param.12), kind=kLoop, calls=%fused_computation.1 | loop fusion | flops 9437184 | bytes 14155776 | tf_op jit(solution)/shard_map/convert_element_type | solution.py:395
  (26 shorter events, 3.3 us)
Async XLA Ops:
  7.2 237.2 %copy-start = (bf16[1536,768]{1,0:T(8,128)(2,1)S(1)}, bf16[1536,768]{1,0:T(8,128)(2,1)}, u32[]{:S(2)}) copy-start(bf16[1536,768]{1,0:T(8,128)(2,1)} %param.23) | copy-start | bytes 7077892
  7.2 172.9 %all-gather.5.cloned.1.call-start = ((), (), s32[]{:S(2)}) async-start(), calls=%async_computation.2 | async-start | bytes 2654208 | tf_op jit(solution)/shard_map/all_gather | solution.py:389
  138.2 47.1 %copy-start.3 = (bf16[24,128,128]{2,1,0:T(8,128)(2,1)}, bf16[24,128,128]{2,1,0:T(8,128)(2,1)S(1)}, u32[]{:S(2)}) copy-start(bf16[24,128,128]{2,1,0:T(8,128)(2,1)S(1)} %get-tuple-element.11) | copy-start | bytes 2359300
  138.9 0.8 copy-start.4
  156.0 80.1 %all-gather.7.cloned.1.call-start = ((), (), s32[]{:S(2)}) async-start(), calls=%async_computation.3 | async-start | bytes 10616832 | tf_op jit(solution)/shard_map/all_gather | solution.py:391
  156.8 210.5 %all-reduce.2.cloned.1.call-start = ((), (), s32[]{:S(2)}) async-start(), calls=%async_computation.1 | async-start | bytes 9437184 | tf_op jit(solution)/shard_map/psum | solution.py:394
  244.4 10.5 %copy-start.2 = (bf16[3072,384]{0,1:T(8,128)(2,1)S(1)}, bf16[3072,384]{0,1:T(8,128)(2,1)}, u32[]{:S(2)}) copy-start(bf16[3072,384]{0,1:T(8,128)(2,1)} %reshape.98) | copy-start | bytes 7077892
  244.4 10.5 %copy-start.5 = (bf16[384,768]{1,0:T(8,128)(2,1)S(1)}, bf16[384,768]{1,0:T(8,128)(2,1)}, u32[]{:S(2)}) copy-start(bf16[384,768]{1,0:T(8,128)(2,1)} %param.22) | copy-start | bytes 1769476
  259.4 115.0 %copy-start.1 = (bf16[1536,768]{1,0:T(8,128)(2,1)S(1)}, bf16[1536,768]{1,0:T(8,128)(2,1)}, u32[]{:S(2)}) copy-start(bf16[1536,768]{1,0:T(8,128)(2,1)} %param.23) | copy-start | bytes 7077892
Sparse Core Ops, SparseCore 0:
  156.1 23.8 all-gather.4
  181.7 54.3 all-gather.6
  259.5 107.7 all-reduce.1

commit v2 on v1

--- a/solution.py
+++ b/solution.py
@@ -11,6 +11,12 @@
 ROPE_BASE = 10000.0
 MESH = pl.DeviceIdType.MESH
 RING = 4
+CORES = 2
+TWO = 2
+LANES = 128
+BOTH = (0, 1)
+KINDS = (0, 1, 2)
+MIB = 2**20
 F32 = jnp.float32
 BF16 = jnp.bfloat16
 
@@ -55,8 +61,8 @@
     pos_p, pos_m, pos_o = (ring_pos + 1) % RING, (ring_pos + RING - 1) % RING, (ring_pos + 2) % RING
     tx_p, tx_m, tx_o = pos_p * 2 + core, pos_m * 2 + core, pos_o * 2 + core
     tx_pair = ring_pos * 2 + other
-    lanes = pl.ds(pl.multiple_of(core * kblk, 128), kblk)
-    krows = pl.ds(pl.multiple_of(core * kblk, 128), kblk)
+    lanes = pl.ds(pl.multiple_of(core * kblk, LANES), kblk)
+    krows = pl.ds(pl.multiple_of(core * kblk, LANES), kblk)
 
     pieces = []
     for d in range(RING):
@@ -75,13 +81,13 @@
     st[...] = jnp.zeros_like(st)
 
     barrier = pltpu.get_barrier_semaphore()
-    pl.semaphore_signal(barrier, inc=1, device_id={"ty": row_idx, "tx": tx_pair}, device_id_type=MESH)
+    pl.semaphore_signal(barrier, device_id={"ty": row_idx, "tx": tx_pair}, device_id_type=MESH)
     for tx in (tx_p, tx_m, tx_o):
-        pl.semaphore_signal(barrier, inc=1, device_id={"ty": row_idx, "tx": tx}, device_id_type=MESH)
+        pl.semaphore_signal(barrier, device_id={"ty": row_idx, "tx": tx}, device_id_type=MESH)
     for off in range(1, ty_size):
-        for cc in range(2):
+        for cc in BOTH:
             pl.semaphore_signal(
-                barrier, inc=1, device_id={"ty": (row_idx + off) % ty_size, "tx": ring_pos * 2 + cc}, device_id_type=MESH
+                barrier, device_id={"ty": (row_idx + off) % ty_size, "tx": ring_pos * 2 + cc}, device_id_type=MESH
             )
     pl.semaphore_wait(barrier, 4 + 2 * (ty_size - 1))
     for swap in swaps:
@@ -96,9 +102,9 @@
 
     def stat_block(b, _):
         def lane_tile(j, sums):
-            part = xs[pl.ds(2 * b, 2), :, pl.ds(pl.multiple_of(j * 128, 128), 128)].reshape(blk, 128).astype(F32)
+            part = xs[pl.ds(2 * b, 2), :, pl.ds(pl.multiple_of(j * 128, LANES), LANES)].reshape(blk, LANES).astype(F32)
             return sums[0] + part, sums[1] + part * part
-        zero = jnp.zeros((blk, 128), F32)
+        zero = jnp.zeros((blk, LANES), F32)
         s1, s2 = lax.fori_loop(0, lane_tiles, lane_tile, (zero, zero))
         st[pl.ds(b, 1), pl.ds(0, blk)] = jnp.sum(s1.T, axis=0, keepdims=True)
         st[pl.ds(b + st.shape[0] // 2, 1), pl.ds(0, blk)] = jnp.sum(s2.T, axis=0, keepdims=True)
@@ -119,13 +125,13 @@
     sr[1, : st.shape[0] // 2, :] = lax.rsqrt(var + EPSILON)
 
     def norm_block(b, _):
-        mean_b = jnp.broadcast_to(sr[0, pl.ds(b, 1), :], (128, 128)).T[:blk]
-        rstd_b = jnp.broadcast_to(sr[1, pl.ds(b, 1), :], (128, 128)).T[:blk]
+        mean_b = jnp.broadcast_to(sr[0, pl.ds(b, 1), :], (128, LANES)).T[:blk]
+        rstd_b = jnp.broadcast_to(sr[1, pl.ds(b, 1), :], (128, LANES)).T[:blk]
         for j in range(lane_tiles):
-            cols = slice(j * 128, (j + 1) * 128)
-            part = xs[pl.ds(2 * b, 2), :, cols].reshape(blk, 128).astype(F32)
+            cols = slice(j * 128, (j + 1) * LANES)
+            part = xs[pl.ds(2 * b, 2), :, cols].reshape(blk, LANES).astype(F32)
             normed = ((part - mean_b) * rstd_b * gam[0:1, cols]).astype(BF16)
-            xs[pl.ds(2 * b, 2), :, cols] = normed.reshape(2, group, 128)
+            xs[pl.ds(2 * b, 2), :, cols] = normed.reshape(2, group, LANES)
         return 0
 
     lax.fori_loop(0, blocks, norm_block, 0)
@@ -165,7 +171,7 @@
 
     def stage_c(s, n, finish):
         w = ws[s, :, 0:n]
-        for half in range(2):
+        for half in BOTH:
             own = mm(ring_pos * half_ty + half * hg, hg, w)
             hop(s, n, 2, half).wait_recv()
             hop(s, n, 1, 1 - half).wait_recv()
@@ -266,13 +272,13 @@
         kv_copy(n, pos).wait_send()
     for swap in swaps:
         swap.wait_send()
-    for kind in range(3):
-        for side in range(2):
+    for kind in KINDS:
+        for side in BOTH:
             hop(0, q_width, kind, side).wait_send()
 
     def drain(s, _):
-        for kind in range(3):
-            for side in range(2):
+        for kind in KINDS:
+            for side in BOTH:
                 hop(s, wide, kind, side).wait_send()
         return 0
 
@@ -283,19 +289,19 @@
 
 def project(x_blk, gamma_blk, wq, wk, wv, wg, wu, cos_q, sin_q, cos_kv, sin_kv, ty_size, seq_block, d_model, tile):
     rows_all, kblk = x_blk.shape
-    half_ty, group = ty_size // 2, 2 * seq_block
+    half_ty, group = ty_size // TWO, TWO * seq_block
     rows = half_ty * group
     q_width, ffn = wq.shape[1], wg.shape[1]
     kv_width = wk.shape[1]
     steps = ffn // tile
     wide = 2 * tile
     kdim = 2 * kblk
-    x_main = x_blk.reshape(2, half_ty, RING, group, kblk)
+    x_main = x_blk.reshape(TWO, half_ty, RING, group, kblk)
     x_kv = x_blk.reshape(ty_size, RING, group, kblk)
     wkv = jnp.stack([wk, wv])
     gamma = jnp.broadcast_to(gamma_blk[None, :], (8, kblk))
     pieces = RING + 4 + 2 * steps
-    stat_lines = 2 * (-(-((RING * half_ty + RING) // 2) // 8) * 8)
+    stat_lines = 2 * (-(-((RING * half_ty + RING) // TWO) // 8) * 8)
     any_spec = pl.BlockSpec(memory_space=pl.ANY)
     vmem_spec = pl.BlockSpec(memory_space=pltpu.VMEM)
     return pl.pallas_call(
@@ -303,7 +309,7 @@
         out_shape=(
             jax.ShapeDtypeStruct((rows, ffn), BF16),
             jax.ShapeDtypeStruct((ty_size, seq_block, q_width), BF16),
-            jax.ShapeDtypeStruct((2, group, kv_width), BF16),
+            jax.ShapeDtypeStruct((TWO, group, kv_width), BF16),
         ),
         in_specs=[any_spec] * 7 + [vmem_spec] * 4,
         out_specs=(any_spec,) * 3,
@@ -312,38 +318,416 @@
             pltpu.VMEM((steps + 1, kdim, wide), BF16),
             pltpu.VMEM((kdim, kv_width), BF16),
             pltpu.VMEM((8, kdim), F32),
-            pltpu.VMEM((stat_lines, 128), F32),
-            pltpu.VMEM((3, stat_lines, 128), F32),
+            pltpu.VMEM((stat_lines, LANES), F32),
+            pltpu.VMEM((3, stat_lines, LANES), F32),
             pltpu.VMEM((steps + 1, rows, wide), BF16),
-            pltpu.VMEM((steps + 1, 2, rows // 2, wide), BF16),
-            pltpu.VMEM((steps + 1, 2, rows // 2, wide), BF16),
-            pltpu.VMEM((steps + 1, 2, rows // 2, wide), BF16),
-            pltpu.VMEM((steps + 1, 2, 2, rows // 2, wide), BF16),
+            pltpu.VMEM((steps + 1, TWO, rows // TWO, wide), BF16),
+            pltpu.VMEM((steps + 1, TWO, rows // TWO, wide), BF16),
+            pltpu.VMEM((steps + 1, TWO, rows // TWO, wide), BF16),
+            pltpu.VMEM((steps + 1, TWO, TWO, rows // TWO, wide), BF16),
             pltpu.VMEM((rows, ffn), BF16),
             pltpu.VMEM((RING, group, kv_width), F32),
             pltpu.VMEM((3, group, kv_width), F32),
-            pltpu.VMEM((2, group, kv_width), BF16),
+            pltpu.VMEM((TWO, group, kv_width), BF16),
             pltpu.VMEM((ty_size, seq_block, q_width), BF16),
             pltpu.VMEM((ty_size, seq_block, q_width), BF16),
             pltpu.SemaphoreType.DMA((pieces,)),
             pltpu.SemaphoreType.DMA((pieces,)),
             pltpu.SemaphoreType.DMA((pieces,)),
-            pltpu.SemaphoreType.DMA((3,)),
-            pltpu.SemaphoreType.DMA((3,)),
-            pltpu.SemaphoreType.DMA((steps + 1, 3, 2)),
-            pltpu.SemaphoreType.DMA((steps + 1, 3, 2)),
-            pltpu.SemaphoreType.DMA((3,)),
-            pltpu.SemaphoreType.DMA((3,)),
-            pltpu.SemaphoreType.DMA((2,)),
+            pltpu.SemaphoreType.DMA((len(KINDS),)),
+            pltpu.SemaphoreType.DMA((len(KINDS),)),
+            pltpu.SemaphoreType.DMA((steps + 1, len(KINDS), TWO)),
+            pltpu.SemaphoreType.DMA((steps + 1, len(KINDS), TWO)),
+            pltpu.SemaphoreType.DMA((len(KINDS),)),
+            pltpu.SemaphoreType.DMA((len(KINDS),)),
+            pltpu.SemaphoreType.DMA((TWO,)),
             pltpu.SemaphoreType.DMA((ty_size,)),
             pltpu.SemaphoreType.DMA((ty_size,)),
-            pltpu.SemaphoreType.DMA((3,)),
+            pltpu.SemaphoreType.DMA((len(KINDS),)),
         ],
         compiler_params=pltpu.CompilerParams(
-            collective_id=0, has_side_effects=True, vmem_limit_bytes=56 * 1024 * 1024
+            collective_id=0, has_side_effects=True, vmem_limit_bytes=56 * MIB
         ),
         name="project",
     )(x_main, x_kv, wq, wkv, wg, wu, gamma, cos_q, sin_q, cos_kv, sin_kv)
+
+
+def combine_kernel(
+    ty_size, chunks,
+    att_in, act_in, x_in, wo, wd,
+    y_out,
+    att, mlp, wos, wds, yp, t1, xr, yf, p2_1, sd_1, sb_1, ra_1, rb_1, p2_2, sd_2, sb_2, ra_2, rb_2,
+    w_sem, wp_send, wp_recv, a2a_send, a2a_recv, mlp_sem, gx_send, gx_recv, x_sem, xp_send, xp_recv,
+    rs_send, rs_recv, ag_send, ag_recv, out_sem, outp_send, outp_recv,
+):
+    row_idx = lax.axis_index("ty")
+    col_idx = lax.axis_index("tx")
+    ring_pos, core = col_idx // 2, col_idx % 2
+    other = 1 - core
+    half_ty = ty_size // 2
+    seq_block = att_in.shape[1]
+    cols = wo.shape[1]
+    hcols = cols // 2
+    pos_p, pos_m = (ring_pos + 1) % RING, (ring_pos + RING - 1) % RING
+    tx_side = (pos_p * 2 + core, pos_m * 2 + core)
+    from_side = (pos_m, pos_p)
+    tx_pair = ring_pos * 2 + other
+    z_pos, y_pos = row_idx // RING, row_idx % RING
+    up = lambda v: (v + 1) % RING
+    down = lambda v: (v + RING - 1) % RING
+    y_side = (z_pos * RING + up(y_pos), z_pos * RING + down(y_pos))
+    z_side = (up(z_pos) * RING + y_pos, down(z_pos) * RING + y_pos)
+    places = ((y_pos, z_pos), (z_pos, y_pos))
+    sides = ((y_side, z_side), (z_side, y_side))
+    blk = yp.shape[1] // RING
+    sub = blk // RING
+    mine = pl.ds(pl.multiple_of(core * cols, LANES), cols)
+
+    def x_tile(c, r):
+        b1, b2 = jnp.where(core == 0, y_pos, z_pos), jnp.where(core == 0, z_pos, y_pos)
+        return x_in.at[c, 2 * r + b2 // 2, b1, b2 % 2]
+
+    w_loads = [pltpu.make_async_copy(wd, wds.at[:, mine], w_sem.at[0]), pltpu.make_async_copy(wo, wos.at[:, mine], w_sem.at[1])]
+    w_swaps = [
+        remote(wd, wds.at[:, mine], wp_send.at[0], wp_recv.at[0], row_idx, tx_pair),
+        remote(wo, wos.at[:, mine], wp_send.at[1], wp_recv.at[1], row_idx, tx_pair),
+    ]
+    mlp_loads = [pltpu.make_async_copy(act_in.at[r], mlp.at[r, ring_pos], mlp_sem.at[r]) for r in range(chunks)]
+    x_loads = [pltpu.make_async_copy(x_tile(core, r), xr.at[core, r], x_sem.at[r]) for r in range(chunks)]
+    x_swaps = [remote(x_tile(other, r), xr.at[core, r], xp_send.at[r], xp_recv.at[r], row_idx, tx_pair) for r in range(chunks)]
+    for load in w_loads + mlp_loads + x_loads:
+        load.start()
+
+    barrier = pltpu.get_barrier_semaphore()
+    pl.semaphore_signal(barrier, device_id={"ty": row_idx, "tx": tx_pair}, device_id_type=MESH)
+    for tx in tx_side:
+        pl.semaphore_signal(barrier, device_id={"ty": row_idx, "tx": tx}, device_id_type=MESH)
+    for off in range(1, ty_size):
+        for cc in BOTH:
+            pl.semaphore_signal(
+                barrier, device_id={"ty": (row_idx + off) % ty_size, "tx": ring_pos * 2 + cc}, device_id_type=MESH
+            )
+    pl.semaphore_wait(barrier, 3 + 2 * (ty_size - 1))
+
+    def gather(r, part, stage, side):
+        sems = gx_send.at[r, part, stage, side], gx_recv.at[r, part, stage, side]
+        buf = (mlp, att)[part]
+        if stage == 0:
+            src = act_in.at[r] if part == 0 else att.at[r, ring_pos]
+            return remote(src, buf.at[r, ring_pos], *sems, row_idx, tx_side[side])
+        block = buf.at[r, from_side[side], side]
+        return remote(block, block, *sems, row_idx, tx_side[side])
+
+    home, home_core = row_idx % half_ty, row_idx // half_ty
+
+    def a2a(k):
+        return remote(
+            att_in.at[k], att.at[home // 2, ring_pos, home % 2, core], a2a_send.at[k], a2a_recv.at[home, core],
+            k, ring_pos * 2 + home_core,
+        )
+
+    def a2a_self(k):
+        return jnp.logical_and(k == row_idx, core == home_core)
+
+    for side in BOTH:
+        gather(0, 0, 0, side).start()
+    for k in range(ty_size):
+        @pl.when(a2a_self(k))
+        def _():
+            pltpu.make_async_copy(
+                att_in.at[k], att.at[home // 2, ring_pos, home % 2, core], a2a_recv.at[home, core]
+            ).start()
+
+        @pl.when(jnp.logical_not(a2a_self(k)))
+        def _():
+            a2a(k).start()
+    for swap in w_swaps + x_swaps:
+        swap.start()
+
+    def att_ready(r):
+        for g in (2 * r, 2 * r + 1):
+            for cc in BOTH:
+                remote(
+                    att_in.at[0], att.at[r, ring_pos, g % 2, cc], a2a_send.at[0], a2a_recv.at[g, cc], row_idx, tx_pair
+                ).wait_recv()
+
+    def own_att(r):
+        att_ready(r)
+        for side in BOTH:
+            gather(r, 1, 0, side).start()
+
+    def own_mlp(r):
+        for side in BOTH:
+            gather(r, 0, 0, side).start()
+
+    def forward(r):
+        for part in BOTH:
+            for side in BOTH:
+                gather(r, part, 0, side).wait_recv()
+                gather(r, part, 1, side).start()
+
+    def multiply(r):
+        mlp_loads[r].wait()
+        for part in BOTH:
+            for side in BOTH:
+                gather(r, part, 1, side).wait_recv()
+        rows = yp.shape[1]
+
+        def tile(n, _):
+            lanes = pl.ds(pl.multiple_of(n * 512, 512), 512)
+            left_mlp = mlp[r].reshape(rows, mlp.shape[-1])
+            left_att = att[r].reshape(rows, att.shape[-1])
+            yp[r, :, lanes] = jnp.dot(left_mlp, wds[:, lanes], preferred_element_type=F32) + jnp.dot(
+                left_att, wos[:, lanes], preferred_element_type=F32
+            )
+            return 0
+
+        lax.fori_loop(0, yp.shape[2] // 512, tile, 0)
+
+    bufs = ((p2_1, sd_1, sb_1, ra_1, rb_1), (p2_2, sd_2, sb_2, ra_2, rb_2))
+
+    def hop(level, r, c, kind, side):
+        p2, sd, sb, ra, rb = bufs[level]
+        src, dst = (
+            (p2.at[r, c, :, pl.ds(side * hcols, hcols)], ra.at[r, c, side]),
+            (sd.at[r, c, side], rb.at[r, c, side, 0]),
+            (sb.at[r, c, side], rb.at[r, c, side, 1]),
+        )[kind]
+        return remote(
+            src, dst, rs_send.at[level, r, c, kind, side], rs_recv.at[level, r, c, kind, side],
+            sides[c][level][side], col_idx,
+        )
+
+    def part_of(level, r, c, b, half):
+        size = (blk, sub)[level]
+        rows = pl.ds(pl.multiple_of(b * size, 8), size)
+        if level == 0:
+            return yp[r, rows, c * cols + half * hcols : c * cols + (half + 1) * hcols]
+        return t1[r, c, rows, half * hcols : (half + 1) * hcols]
+
+    def reduce_a(level, r):
+        p2, sd = bufs[level][:2]
+        for c in BOTH:
+            pos = places[c][level]
+            for half in BOTH:
+                p2[r, c, :, half * hcols : (half + 1) * hcols] = part_of(level, r, c, (pos + 2) % RING, half).astype(BF16)
+                hop(level, r, c, 0, half).start()
+        for c in BOTH:
+            pos = places[c][level]
+            sd[r, c, 0] = part_of(level, r, c, up(pos), 1).astype(BF16)
+            hop(level, r, c, 1, 0).start()
+            sd[r, c, 1] = part_of(level, r, c, down(pos), 0).astype(BF16)
+            hop(level, r, c, 1, 1).start()
+
+    def reduce_b(level, r):
+        sb, ra = bufs[level][2:4]
+        for c in BOTH:
+            pos = places[c][level]
+            for side, b in ((0, up(pos)), (1, down(pos))):
+                hop(level, r, c, 0, side).wait_recv()
+                sb[r, c, side] = (part_of(level, r, c, b, side) + ra[r, c, side].astype(F32)).astype(BF16)
+                hop(level, r, c, 2, side).start()
+
+    def reduce_c(level, r, finish):
+        rb = bufs[level][4]
+        for c in BOTH:
+            pos = places[c][level]
+            for half in BOTH:
+                hop(level, r, c, 1, 1 - half).wait_recv()
+                hop(level, r, c, 2, half).wait_recv()
+                finish(
+                    c, half,
+                    part_of(level, r, c, pos, half) + rb[r, c, half, 1].astype(F32) + rb[r, c, 1 - half, 0].astype(F32),
+                )
+
+    def spread(level, r, c, stage, side):
+        ring, (p1, p2) = sides[c][level], places[c]
+        sems = ag_send.at[level, r, c, stage, side], ag_recv.at[level, r, c, stage, side]
+        near = (down, up)[side]
+        if level == 1:
+            if stage == 0:
+                block = yf.at[r, c, p1, p2 // 2, p2 % 2]
+            else:
+                block = yf.at[r, c, p1, near(p2) // 2, near(p2) % 2, :, pl.ds(side * hcols, hcols)]
+        elif stage == 0:
+            block = yf.at[r, c, p1]
+        else:
+            block = yf.at[r, c, near(p1), side]
+        return remote(block, block, *sems, ring[side], col_idx)
+
+    def spread_own(level, r):
+        for c in BOTH:
+            for side in BOTH:
+                spread(level, r, c, 0, side).start()
+
+    def spread_on(level, r):
+        for c in BOTH:
+            for side in BOTH:
+                spread(level, r, c, 0, side).wait_recv()
+                spread(level, r, c, 1, side).start()
+
+    def spread_end(level, r):
+        for c in BOTH:
+            for side in BOTH:
+                spread(level, r, c, 1, side).wait_recv()
+
+    def s3(r):
+        reduce_b(0, r)
+
+    def s4(r):
+        def finish(c, half, vals):
+            t1[r, c, :, half * hcols : (half + 1) * hcols] = vals
+        reduce_c(0, r, finish)
+        reduce_a(1, r)
+
+    def s5(r):
+        reduce_b(1, r)
+
+    def s6(r):
+        x_loads[r].wait()
+        remote(x_tile(other, r), xr.at[other, r], xp_send.at[r], xp_recv.at[r], row_idx, tx_pair).wait_recv()
+
+        def finish(c, half, vals):
+            lanes = slice(half * hcols, (half + 1) * hcols)
+            p1, p2 = places[c]
+            yf[r, c, p1, p2 // 2, p2 % 2, :, lanes] = (xr[c, r, :, lanes].astype(F32) + vals).astype(BF16)
+        reduce_c(1, r, finish)
+        spread_own(1, r)
+
+    def s7(r):
+        spread_on(1, r)
+
+    def s8(r):
+        spread_end(1, r)
+        spread_own(0, r)
+
+    def s9(r):
+        spread_on(0, r)
+
+    def out_copy(r, p):
+        return pltpu.make_async_copy(
+            yf.at[r, core, p], y_out.at[core, pl.ds(2 * r, 2), p], out_sem.at[r, p]
+        )
+
+    def out_swap(r, p):
+        return remote(
+            yf.at[r, other, p], y_out.at[core, pl.ds(2 * r, 2), p],
+            outp_send.at[r, p], outp_recv.at[r, p], row_idx, tx_pair,
+        )
+
+    def s10(r):
+        spread_end(0, r)
+        for p in range(RING):
+            out_swap(r, p).start()
+            out_copy(r, p).start()
+
+    def s2(r):
+        multiply(r)
+        reduce_a(0, r)
+
+    own_mlp(1)
+    own_att(0)
+    own_att(1)
+    forward(0)
+    own_mlp(2)
+    own_att(2)
+    forward(1)
+    own_mlp(3)
+    own_att(3)
+    for n in BOTH:
+        w_loads[n].wait()
+        w_swaps[n].wait_recv()
+    stages = (s2, s3, s4, s5, s6, s7, s8, s9, s10)
+    first = (0, 4, 8, 9)
+    for tick in range(first[-1] + len(stages)):
+        for r in range(chunks):
+            n = tick - first[r]
+            if 0 <= n < len(stages):
+                stages[n](r)
+        if tick == first[1] - 1:
+            forward(2)
+        if tick == first[2] - 1:
+            forward(3)
+
+    for swap in w_swaps + x_swaps:
+        swap.wait_send()
+    for k in range(ty_size):
+        @pl.when(jnp.logical_not(a2a_self(k)))
+        def _():
+            a2a(k).wait_send()
+    for r in range(chunks):
+        for a in BOTH:
+            for b in BOTH:
+                for side in BOTH:
+                    gather(r, a, b, side).wait_send()
+                    for level in BOTH:
+                        spread(level, r, a, b, side).wait_send()
+        for level in BOTH:
+            for c in BOTH:
+                for kind in KINDS:
+                    for side in BOTH:
+                        hop(level, r, c, kind, side).wait_send()
+        for p in range(RING):
+            out_copy(r, p).wait()
+            out_swap(r, p).wait()
+
+
+def combine(att_owned, act_own, x_blk, w_out, w_down, ty_size):
+    seq_block = att_owned.shape[1]
+    chunks = ty_size // 4
+    group, half_ty = 2 * seq_block, ty_size // 2
+    cols = w_out.shape[1]
+    per = half_ty // chunks
+    ffn, q_width = w_down.shape[0], w_out.shape[0]
+    crows = RING * per * group
+    blk, sub, hcols = crows // RING, crows // RING // RING, cols // 2
+    any_spec = pl.BlockSpec(memory_space=pl.ANY)
+    ring_bufs = []
+    for m in (blk, sub):
+        ring_bufs += [
+            pltpu.VMEM((chunks, TWO, m, cols), BF16),
+            pltpu.VMEM((chunks, TWO, TWO, m, hcols), BF16),
+            pltpu.VMEM((chunks, TWO, TWO, m, hcols), BF16),
+            pltpu.VMEM((chunks, TWO, TWO, m, hcols), BF16),
+            pltpu.VMEM((chunks, TWO, TWO, TWO, m, hcols), BF16),
+        ]
+    dma = pltpu.SemaphoreType.DMA
+    y = pl.pallas_call(
+        functools.partial(combine_kernel, ty_size, chunks),
+        out_shape=jax.ShapeDtypeStruct((TWO, half_ty, RING, TWO, seq_block, cols), BF16),
+        in_specs=[any_spec] * 5,
+        out_specs=any_spec,
+        scratch_shapes=[
+            pltpu.VMEM((chunks, RING, per, TWO, seq_block, q_width), BF16),
+            pltpu.VMEM((chunks, RING, per, group, ffn), BF16),
+            pltpu.VMEM((q_width, TWO * cols), BF16),
+            pltpu.VMEM((ffn, TWO * cols), BF16),
+            pltpu.VMEM((chunks, crows, TWO * cols), F32),
+            pltpu.VMEM((chunks, TWO, blk, cols), F32),
+            pltpu.VMEM((TWO, chunks, seq_block, cols), BF16),
+            pltpu.VMEM((chunks, TWO, RING, TWO, TWO, seq_block, cols), BF16),
+            *ring_bufs,
+            dma((CORES,)), dma((CORES,)), dma((CORES,)),
+            dma((ty_size,)), dma((half_ty, TWO)),
+            dma((chunks,)),
+            dma((chunks, TWO, TWO, TWO)), dma((chunks, TWO, TWO, TWO)),
+            dma((chunks,)), dma((chunks,)), dma((chunks,)),
+            dma((TWO, chunks, TWO, len(KINDS), TWO)), dma((TWO, chunks, TWO, len(KINDS), TWO)),
+            dma((TWO, chunks, TWO, TWO, TWO)), dma((TWO, chunks, TWO, TWO, TWO)),
+            dma((chunks, RING)), dma((chunks, RING)), dma((chunks, RING)),
+        ],
+        compiler_params=pltpu.CompilerParams(
+            collective_id=1, has_side_effects=True, vmem_limit_bytes=60 * MIB
+        ),
+        name="combine",
+    )(
+        att_owned,
+        act_own.reshape(chunks, per, group, ffn),
+        x_blk.reshape(TWO, half_ty, RING, TWO, seq_block, cols),
+        w_out,
+        w_down,
+    )
+    return y.reshape(x_blk.shape)
 
 
 def solution(mesh):
@@ -385,14 +769,8 @@
         scores = jnp.where(in_range, scores, -1e30)
         att_probs = jax.nn.softmax(scores, axis=-1).astype(BF16)
         att_owned = jnp.einsum("gbht,btd->gbhd", att_probs, v_out, preferred_element_type=F32).astype(BF16)
-        att_column = lax.all_to_all(att_owned, "ty", 0, 0, tiled=True)
-        att_rows = lax.all_gather(att_column, "tx", axis=1, tiled=False).reshape(rows, local_heads * head_dim)
-
-        mlp_all = lax.all_gather(act_own, "tx", axis=0, tiled=False)
-        mlp_act = mlp_all.reshape(RING, 2, half_ty, group, -1).transpose(1, 2, 0, 3, 4).reshape(rows, -1)
-        part_out = jnp.dot(att_rows, w_out, preferred_element_type=F32) + jnp.dot(mlp_act, w_down, preferred_element_type=F32)
-        out_sum = lax.psum(part_out.astype(BF16), "ty")
-        y_blk = (x_blk.astype(F32) + out_sum.astype(F32)).astype(BF16)
+        att_owned = att_owned.reshape(ty_size, seq_block, local_heads * head_dim)
+        y_blk = combine(att_owned, act_own, x_blk, w_out, w_down, ty_size)
         return y_blk, k_out, v_out
 
     in_specs = (P("dp", "tx"), P("dp"), cache_spec, cache_spec, P("tx"), P("tx", "ty"), P("tx", None), P("tx", None), P("tx", "ty"), P("tx", "ty"), P("ty", "tx"), P("ty", "tx"))

time: 382 us -> 256 us (0.67)
  waiting for transfers between devices: 176 us -> 0 us
  Pallas kernels: 118 us -> 232 us
  matrix products: 19.2 us -> 3.39 us
  local copies, waits for them, and re-layouts: 26.5 us -> 10.9 us
  between operations: 13.9 us -> 0.81 us
  blocking collectives: 11.4 us -> 0 us
  other arithmetic: 15.2 us -> 7.54 us
    pallas_call x0 -> x1, Pallas kernels: none -> 114 us  [combine(): pl.pallas_call(functools.partial(combine_kernel, ty_size, chunks), out_sh...]
    psum x1 -> x0, waiting for transfers between devices: 108 us -> none  [layer_shard(): out_sum = lax.psum(part_out.astype(BF16), 'ty')]
    all_gather x2 -> x0, waiting for transfers between devices: 67.6 us -> none  [the longest x1 44.6 us: layer_shard(): mlp_all = lax.all_gather(act_own, 'tx', axis=0, tiled=False)]
    dot_general x2 -> x0, matrix products: 14.9 us -> none  [the longest x1 10.5 us: layer_shard(): jnp.dot(mlp_act, w_down, preferred_element_type=F32)]
    reshape x2 -> x1, local copies, waits for them, and re-layouts: 14.4 us -> 0.97 us  [layer_shard(): att_owned = att_owned.reshape(ty_size, seq_block, local_heads * head_dim)]
    all_to_all x1 -> x0, blocking collectives: 11.4 us -> none  [layer_shard(): att_column = lax.all_to_all(att_owned, 'ty', 0, 0, tiled=True)]
    convert_element_type x1 -> x0, other arithmetic: 7.15 us -> none  [layer_shard(): y_blk = (x_blk.astype(F32) + out_sum.astype(F32)).astype(BF16)]
    all_gather x1 -> x0, local copies, waits for them, and re-layouts: 5.33 us -> none  [layer_shard(): lax.all_gather(att_column, 'tx', axis=1, tiled=False)]
  transfers between devices with their start and end apart: 3 -> 0, of which waited for: 3 -> 0; matrix products, arithmetic and copies ran while one was open for 3% -> 0% of each run, Pallas kernels for 0% -> 0%
where the time goes in v2:
time: 256 us; the launch traced here: 255 us
  Pallas kernels  232 us (91%)
  local copies, waits for them, and re-layouts  10.9 us (4%)
  other arithmetic  7.54 us (3%)
  matrix products  3.39 us (1%)
    pallas_call x1, Pallas kernels, project(): pl.pallas_call(functools.partial(project_kernel, ty_size, tile, d_model),...  118 us
    pallas_call x1, Pallas kernels, combine(): pl.pallas_call(functools.partial(combine_kernel, ty_size, chunks), out_sh...  114 us

profile of v2, /device:TPU:1, one launch (start us, length us, event | category | flops | bytes accessed | tf_op | source)
XLA Modules:
  0.0 255.1 jit_solution(7971700287884924134)
XLA Ops:
  0.7 0.8 fusion.12
  1.5 0.8 dynamic_slice.12
  2.2 0.7 iota_compare_fusion
  2.9 1.3 broadcast_in_dim.61.gamma
  4.2 0.8 reshape.99
  5.0 0.1 convert_element_type.23
  5.1 0.2 fusion.11
  5.3 0.7 pad_maximum_fusion.3
  6.0 1.8 pad_maximum_fusion.wkv
  7.8 0.8 fusion.10
  8.6 0.9 pad_maximum_fusion.1
  9.5 118.2 %project.1 = (bf16[384,1536]{1,0:T(8,128)(2,1)}, bf16[16,24,384]{2,1,0:T(8,128)(2,1)}, bf16[2,48,128]{2,1,0:T(8,128)(2,1)}) custom-call(bf16[2,8,4,48,768]{4,3,2,1,0:T(8,128)(2,1)} %bitcast.27, bf16[16,4,48,768]{3,2,1,0:T(8,128)(2,1)} %bitcast.28, bf16[768,384]{1,0:T(8,128)(2,1)} %wq.1, bf16[2,768,128]{2,1,0:T(8,128)(2,1)} %pad_maximum_fusion.wkv, ...), custom_call_target="tpu_custom_call" | custom-call | tf_op jit(solution)/shard_map/project/pallas_call | solution.py:307
  127.7 0.7 dynamic-slice_bitcast_fusion
  128.4 1.3 reshape.100
  129.8 1.3 broadcast_select_fusion
  131.1 0.0 copy-start
  131.1 0.0 copy-start.3
  131.1 1.4 fusion.3
  132.4 0.4 fusion.14
  132.9 2.0 fusion.5
  134.9 0.2 copy.18
  135.1 1.0 reshape.101.att_in
  136.1 114.2 %combine.1 = bf16[2,8,4,2,24,768]{5,4,3,2,1,0:T(8,128)(2,1)} custom-call(bf16[16,24,384]{2,1,0:T(8,128)(2,1)} %reshape.101.att_in, bf16[4,2,48,1536]{3,2,1,0:T(8,128)(2,1)} %bitcast.31, bf16[2,8,4,2,24,768]{5,4,3,2,1,0:T(8,128)(2,1)} %bitcast.29, bf16[384,768]{1,0:T(8,128)(2,1)} %wo.1, bf16[1536,768]{1,0:T(8,128)(2,1)} %wd.1), custom_call_target="tpu_custom_call" | custom-call | tf_op jit(solution)/shard_map/combine/pallas_call | solution.py:695
  250.3 4.8 %copy.24 = bf16[3072,768]{1,0:T(8,128)(2,1)} copy(bf16[3072,768]{1,0:T(8,128)(2,1)} %bitcast.30) | data formatting | bytes 9437184
  (8 shorter events, 0.0 us)
Async XLA Ops:
  9.5 120.3 %copy-start.1 = (bf16[24,128,128]{2,1,0:T(8,128)(2,1)S(1)}, bf16[24,128,128]{2,1,0:T(8,128)(2,1)}, u32[]{:S(2)}) copy-start(bf16[24,128,128]{2,1,0:T(8,128)(2,1)} %param.14) | copy-start | bytes 2359300
  9.5 120.3 %copy-start.2 = (bf16[24,128,128]{2,1,0:T(8,128)(2,1)S(1)}, bf16[24,128,128]{2,1,0:T(8,128)(2,1)}, u32[]{:S(2)}) copy-start(bf16[24,128,128]{2,1,0:T(8,128)(2,1)} %param.15) | copy-start | bytes 2359300
  131.1 3.9 %copy-start = (bf16[24,128,128]{2,1,0:T(8,128)(2,1)}, bf16[24,128,128]{2,1,0:T(8,128)(2,1)S(1)}, u32[]{:S(2)}) copy-start(bf16[24,128,128]{2,1,0:T(8,128)(2,1)S(1)} %get-tuple-element.29) | copy-start | bytes 2359300
  131.1 3.8 %copy-start.3 = (bf16[24,128,128]{2,1,0:T(8,128)(2,1)}, bf16[24,128,128]{2,1,0:T(8,128)(2,1)S(1)}, u32[]{:S(2)}) copy-start(bf16[24,128,128]{2,1,0:T(8,128)(2,1)S(1)} %get-tuple-element.30) | copy-start | bytes 2359300

commit v3 on v2

--- a/solution.py
+++ b/solution.py
@@ -17,16 +17,15 @@
 BOTH = (0, 1)
 KINDS = (0, 1, 2)
 MIB = 2**20
+ORDER = "2030400250216003317041802251902332611033427143" + "528153629163721173828392931213"
 F32 = jnp.float32
 BF16 = jnp.bfloat16
 
 
-def rope_tables(positions, head_dim):
+def inverse_freqs(head_dim):
     half_dim = head_dim // 2
-    inv_freqs = ROPE_BASE ** (-(jnp.arange(half_dim, dtype=F32) * 2.0) / head_dim)
-    angles = positions.astype(F32)[:, None] * inv_freqs[None, :]
-    cosines, sines = jnp.cos(angles), jnp.sin(angles)
-    return jnp.concatenate([cosines, cosines], axis=-1), jnp.concatenate([-sines, sines], axis=-1)
+    freqs = ROPE_BASE ** (-(jnp.arange(half_dim, dtype=F32) * 2.0) / head_dim)
+    return jnp.concatenate([freqs, freqs])[None, :]
 
 
 def remote(src, dst, send_sem, recv_sem, ty, tx):
@@ -38,7 +37,7 @@
 
 def project_kernel(
     ty_size, tile, d_model,
-    x_main, x_kv, wq, wkv, wg, wu, gamma, cos_q, sin_q, cos_kv, sin_kv,
+    x_main, x_kv, wq, wk, wv, wg, wu, gamma, lens, freqs,
     act_out, q_out, kv_out,
     xs, ws, wkvs, gam, st, sr, p2, sd, sb, ra, rb, act, kvs, kvr, kvf, qs, qr,
     load_sem, pair_send, pair_recv, st_send, st_recv, ssem, rsem, kv_ssem, kv_rsem, kvf_sem, q_ssem, q_rsem, out_sem,
@@ -56,7 +55,7 @@
     kdim = xs.shape[2]
     kblk = kdim // 2
     steps = wg.shape[1] // tile
-    head_dim = cos_q.shape[1]
+    head_dim = freqs.shape[1]
     q_width = wq.shape[1]
     pos_p, pos_m, pos_o = (ring_pos + 1) % RING, (ring_pos + RING - 1) % RING, (ring_pos + 2) % RING
     tx_p, tx_m, tx_o = pos_p * 2 + core, pos_m * 2 + core, pos_o * 2 + core
@@ -70,14 +69,22 @@
     pieces.append((lambda c: x_kv.at[row_idx], xs.at[pl.ds(RING * half_ty, RING), :, lanes]))
     pieces.append((lambda c: gamma, gam.at[:, lanes]))
     pieces.append((lambda c: wq, ws.at[0, krows, pl.ds(0, q_width)]))
-    pieces.append((lambda c: wkv.at[c], wkvs.at[krows]))
+    kv_piece = len(pieces)
+    pieces.append((lambda c: wk, wkvs.at[krows]))
     for t in range(steps):
         pieces.append((lambda c, t=t: wg.at[:, pl.ds(t * tile, tile)], ws.at[t + 1, krows, pl.ds(0, tile)]))
         pieces.append((lambda c, t=t: wu.at[:, pl.ds(t * tile, tile)], ws.at[t + 1, krows, pl.ds(tile, tile)]))
     loads = [pltpu.make_async_copy(src(core), dst, load_sem.at[n]) for n, (src, dst) in enumerate(pieces)]
     swaps = [remote(src(other), dst, pair_send.at[n], pair_recv.at[n], row_idx, tx_pair) for n, (src, dst) in enumerate(pieces)]
-    for load in loads:
-        load.start()
+    def start(copies, kv_copies, wants):
+        for n, copy in enumerate(copies):
+            if n != kv_piece:
+                copy.start()
+            else:
+                for which in BOTH:
+                    pl.when(wants == which)(kv_copies[which].start)
+
+    start(loads, [pltpu.make_async_copy(w, wkvs.at[krows], load_sem.at[kv_piece]) for w in (wk, wv)], core)
     st[...] = jnp.zeros_like(st)
 
     barrier = pltpu.get_barrier_semaphore()
@@ -90,27 +97,36 @@
                 barrier, device_id={"ty": (row_idx + off) % ty_size, "tx": ring_pos * 2 + cc}, device_id_type=MESH
             )
     pl.semaphore_wait(barrier, 4 + 2 * (ty_size - 1))
-    for swap in swaps:
-        swap.start()
-    for n in range(6):
-        loads[n].wait()
-        swaps[n].wait_recv()
+    kv_swaps = [
+        remote(w, wkvs.at[krows], pair_send.at[kv_piece], pair_recv.at[kv_piece], row_idx, tx_pair) for w in (wk, wv)
+    ]
+    start(swaps, kv_swaps, other)
 
     blk = 2 * group
     blocks = (RING * half_ty + RING) // 2
     lane_tiles = kdim // 128
 
-    def stat_block(b, _):
-        def lane_tile(j, sums):
-            part = xs[pl.ds(2 * b, 2), :, pl.ds(pl.multiple_of(j * 128, LANES), LANES)].reshape(blk, LANES).astype(F32)
-            return sums[0] + part, sums[1] + part * part
-        zero = jnp.zeros((blk, LANES), F32)
-        s1, s2 = lax.fori_loop(0, lane_tiles, lane_tile, (zero, zero))
-        st[pl.ds(b, 1), pl.ds(0, blk)] = jnp.sum(s1.T, axis=0, keepdims=True)
-        st[pl.ds(b + st.shape[0] // 2, 1), pl.ds(0, blk)] = jnp.sum(s2.T, axis=0, keepdims=True)
-        return 0
-
-    lax.fori_loop(0, blocks, stat_block, 0)
+    def add_stats(slab):
+        def stat_block(b, _):
+            def lane_tile(j, sums):
+                tile_lanes = pl.ds(pl.multiple_of(slab * kblk + j * LANES, LANES), LANES)
+                part = xs[pl.ds(2 * b, 2), :, tile_lanes].reshape(blk, LANES).astype(F32)
+                return sums[0] + part, sums[1] + part * part
+            zero = jnp.zeros((blk, LANES), F32)
+            sums = lax.fori_loop(0, kblk // LANES, lane_tile, (zero, zero))
+            for which in BOTH:
+                line = pl.ds(b + which * (st.shape[0] // 2), 1)
+                st[line, pl.ds(0, blk)] += jnp.sum(sums[which].T, axis=0, keepdims=True)
+            return 0
+
+        lax.fori_loop(0, blocks, stat_block, 0)
+
+    for n in range(kv_piece - 1):
+        loads[n].wait()
+    add_stats(core)
+    for n in range(kv_piece - 1):
+        swaps[n].wait_recv()
+    add_stats(other)
     stat_copies = [
         remote(st, sr.at[n], st_send.at[n], st_recv.at[n], row_idx, tx) for n, tx in enumerate((tx_p, tx_m, tx_o))
     ]
@@ -134,7 +150,11 @@
             xs[pl.ds(2 * b, 2), :, cols] = normed.reshape(2, group, LANES)
         return 0
 
-    lax.fori_loop(0, blocks, norm_block, 0)
+    per_dest = half_ty // 2
+
+    def norm_dest(d, count):
+        lax.fori_loop(d * per_dest, d * per_dest + count, norm_block, 0)
+
 
     def left(start, count):
         return xs[pl.ds(start, count)].reshape(count * group, kdim)
@@ -151,15 +171,22 @@
         )[kind]
         return remote(src, dst, ssem.at[s, kind, side], rsem.at[s, kind, side], row_idx, (tx_p, tx_m)[side])
 
-    def stage_a(s, n):
+    def stage_far(s, n):
         w = ws[s, :, 0:n]
         p2[s, :, 0:n] = mm(pos_o * half_ty, half_ty, w).astype(BF16)
         hop(s, n, 0, 0).start()
         hop(s, n, 0, 1).start()
+
+    def stage_near(s, n):
+        w = ws[s, :, 0:n]
         sd[s, 0, :, 0:n] = mm(pos_p * half_ty + hg, hg, w).astype(BF16)
         hop(s, n, 1, 0).start()
         sd[s, 1, :, 0:n] = mm(pos_m * half_ty, hg, w).astype(BF16)
         hop(s, n, 1, 1).start()
+
+    def stage_a(s, n):
+        stage_far(s, n)
+        stage_near(s, n)
 
     def stage_b(s, n):
         w = ws[s, :, 0:n]
@@ -177,16 +204,24 @@
             hop(s, n, 1, 1 - half).wait_recv()
             finish(half, own + rb[s, half, 1, :, 0:n].astype(F32) + rb[s, 1 - half, 0, :, 0:n].astype(F32))
 
+    low = lax.broadcasted_iota(jnp.int32, (group, head_dim), 1) < head_dim // 2
+
+    def tables(positions):
+        angles = jnp.broadcast_to(positions.astype(F32), (head_dim, group)).T * freqs[...]
+        sines = jnp.sin(angles)
+        return jnp.cos(angles), jnp.where(low, -sines, sines)
+
     def turn(vals, cos2, sin2):
         return vals * cos2 + pltpu.roll(vals, head_dim // 2, 1) * sin2
 
     def finish_q(half, vals):
-        tab = pl.ds(half * hrows, hrows)
-        for h in range(q_width // head_dim):
-            cols = slice(h * head_dim, (h + 1) * head_dim)
-            turned = turn(vals[:, cols], cos_q[tab, :], sin_q[tab, :])
-            for k in range(2 * hg):
-                qs[half * 2 * hg + k, :, cols] = turned[k * seq_block : (k + 1) * seq_block].astype(BF16)
+        for g in range(hg):
+            cos2, sin2 = tables(lens[pl.ds((core * half_ty + half * hg + g) * RING + ring_pos, 1), :])
+            for h in range(q_width // head_dim):
+                cols = slice(h * head_dim, (h + 1) * head_dim)
+                turned = turn(vals[g * group : (g + 1) * group, cols], cos2, sin2).astype(BF16)
+                for k in BOTH:
+                    qs[2 * (half * hg + g) + k, :, cols] = turned[k * seq_block : (k + 1) * seq_block]
 
     def finish_mlp(s):
         def finish(half, vals):
@@ -210,15 +245,20 @@
         return remote(kvs.at[pos], kvr.at[n], kv_ssem.at[n], kv_rsem.at[n], row_idx, pos * 2 + core)
 
     wide = 2 * tile
-    loads[6].wait()
-    swaps[6].wait_recv()
-    stage_a(0, q_width)
-    loads[7].wait()
-    swaps[7].wait_recv()
+    norm_dest(pos_o, per_dest)
+    for n in (kv_piece - 1, kv_piece):
+        loads[n].wait()
+        swaps[n].wait_recv()
+    stage_far(0, q_width)
+    norm_dest(pos_p, per_dest)
+    norm_dest(pos_m, per_dest)
+    stage_near(0, q_width)
+    norm_dest(RING, 2)
     kvs[...] = mm(RING * half_ty, RING, wkvs[...]).reshape(kvs.shape)
     for n, pos in enumerate((pos_p, pos_m, pos_o)):
         kv_copy(n, pos).start()
-    for n in range(8, len(loads)):
+    norm_dest(ring_pos, per_dest)
+    for n in range(kv_piece + 1, len(loads)):
         loads[n].wait()
         swaps[n].wait_recv()
     stage_a(1, wide)
@@ -226,7 +266,7 @@
     for n, pos in enumerate((pos_p, pos_m, pos_o)):
         kv_copy(n, pos).wait_recv()
     new_row = (kvs[ring_pos] + kvr[0]) + (kvr[1] + kvr[2])
-    kvf[core] = turn(new_row, cos_kv[...], sin_kv[...]).astype(BF16)
+    kvf[core] = turn(new_row, *tables(lens[pl.ds(row_idx * RING + ring_pos, 1), :] * other)).astype(BF16)
     kv_pair = remote(kvf.at[core], kvf.at[core], kvf_sem.at[0], kvf_sem.at[1], row_idx, tx_pair)
     kv_pair.start()
     stage_a(2, wide)
@@ -287,7 +327,7 @@
         out.wait()
 
 
-def project(x_blk, gamma_blk, wq, wk, wv, wg, wu, cos_q, sin_q, cos_kv, sin_kv, ty_size, seq_block, d_model, tile):
+def project(x_blk, gamma_blk, wq, wk, wv, wg, wu, lens, head_dim, ty_size, seq_block, d_model, tile):
     rows_all, kblk = x_blk.shape
     half_ty, group = ty_size // TWO, TWO * seq_block
     rows = half_ty * group
@@ -298,8 +338,6 @@
     kdim = 2 * kblk
     x_main = x_blk.reshape(TWO, half_ty, RING, group, kblk)
     x_kv = x_blk.reshape(ty_size, RING, group, kblk)
-    wkv = jnp.stack([wk, wv])
-    gamma = jnp.broadcast_to(gamma_blk[None, :], (8, kblk))
     pieces = RING + 4 + 2 * steps
     stat_lines = 2 * (-(-((RING * half_ty + RING) // TWO) // 8) * 8)
     any_spec = pl.BlockSpec(memory_space=pl.ANY)
@@ -311,13 +349,13 @@
             jax.ShapeDtypeStruct((ty_size, seq_block, q_width), BF16),
             jax.ShapeDtypeStruct((TWO, group, kv_width), BF16),
         ),
-        in_specs=[any_spec] * 7 + [vmem_spec] * 4,
+        in_specs=[any_spec] * 8 + [vmem_spec] * 2,
         out_specs=(any_spec,) * 3,
         scratch_shapes=[
             pltpu.VMEM((RING * half_ty + RING, group, kdim), BF16),
             pltpu.VMEM((steps + 1, kdim, wide), BF16),
             pltpu.VMEM((kdim, kv_width), BF16),
-            pltpu.VMEM((8, kdim), F32),
+            pltpu.VMEM((1, kdim), F32),
             pltpu.VMEM((stat_lines, LANES), F32),
             pltpu.VMEM((3, stat_lines, LANES), F32),
             pltpu.VMEM((steps + 1, rows, wide), BF16),
@@ -349,7 +387,9 @@
             collective_id=0, has_side_effects=True, vmem_limit_bytes=56 * MIB
         ),
         name="project",
-    )(x_main, x_kv, wq, wkv, wg, wu, gamma, cos_q, sin_q, cos_kv, sin_kv)
+    )(
+        x_main, x_kv, wq, wk, wv, wg, wu, gamma_blk[None, :], lens.reshape(-1, group), inverse_freqs(head_dim)
+    )
 
 
 def combine_kernel(
@@ -637,17 +677,9 @@
     for n in BOTH:
         w_loads[n].wait()
         w_swaps[n].wait_recv()
-    stages = (s2, s3, s4, s5, s6, s7, s8, s9, s10)
-    first = (0, 4, 8, 9)
-    for tick in range(first[-1] + len(stages)):
-        for r in range(chunks):
-            n = tick - first[r]
-            if 0 <= n < len(stages):
-                stages[n](r)
-        if tick == first[1] - 1:
-            forward(2)
-        if tick == first[2] - 1:
-            forward(3)
+    stages = (forward, s10, s2, s3, s4, s5, s6, s7, s8, s9)
+    for stage, r in zip(ORDER[0::TWO], ORDER[1::TWO]):
+        stages[int(stage)](int(r))
 
     for swap in w_swaps + x_swaps:
         swap.wait_send()
@@ -739,22 +771,16 @@
         rows = x_blk.shape[0]
         d_model = x_blk.shape[1] * tx_size
         seq_block, ctx_len, head_dim = k_blk.shape
-        half_ty, group = ty_size // 2, 2 * seq_block
         local_heads = w_query.shape[1] // head_dim
         row_idx = lax.axis_index("ty")
         col_idx = lax.axis_index("tx")
         ring_pos, core = col_idx // 2, col_idx % 2
         tile = min(256, w_gate.shape[1])
 
-        lens_q = lax.dynamic_slice(lens_part.reshape(2, half_ty, RING, group), (core, 0, ring_pos, 0), (1, half_ty, 1, group))
-        cos_q, sin_q = rope_tables(lens_q.reshape(-1), head_dim)
         block_start = (row_idx * tx_size + col_idx) * seq_block
         lens_own = lax.dynamic_slice_in_dim(lens_part, block_start, seq_block)
-        lens_kv = lax.dynamic_slice_in_dim(lens_part, (row_idx * RING + ring_pos) * group, group)
-        cos_kv, sin_kv = rope_tables(jnp.where(core == 0, lens_kv, 0), head_dim)
-
         act_own, q_owned, kv_new = project(
-            x_blk, gamma_blk, w_query, w_key, w_value, w_gate, w_up, cos_q, sin_q, cos_kv, sin_kv,
+            x_blk, gamma_blk, w_query, w_key, w_value, w_gate, w_up, lens_part, head_dim,
             ty_size, seq_block, d_model, tile,
         )
         kv_own = lax.dynamic_slice_in_dim(kv_new, core * seq_block, seq_block, axis=1)

time: 256 us -> 235 us (0.918)
  Pallas kernels: 232 us -> 216 us
  other arithmetic: 7.54 us -> 2.97 us
    pallas_call x1, Pallas kernels: 114 us -> 102 us  [combine(): pl.pallas_call(functools.partial(combine_kernel, ty_size, chunks), out_sh...]
    pallas_call x1, Pallas kernels: 118 us -> 114 us  [project(): pl.pallas_call(functools.partial(project_kernel, ty_size, tile, d_model),...]
where the time goes in v3:
time: 235 us
  Pallas kernels  216 us (92%)
  local copies, waits for them, and re-layouts  11.4 us (5%)
  matrix products  3.41 us (1%)
  other arithmetic  2.97 us (1%)
    pallas_call x1, Pallas kernels, project(): pl.pallas_call(functools.partial(project_kernel, ty_size, tile, d_model),...  114 us
    pallas_call x1, Pallas kernels, combine(): pl.pallas_call(functools.partial(combine_kernel, ty_size, chunks), out_sh...  102 us
    unnamed x9, local copies, waits for them, and re-layouts  4.85 us

profile of v3, /device:TPU:1, one launch (start us, length us, event | category | flops | bytes accessed | tf_op | source)
XLA Modules:
  0.0 234.9 jit_solution(13222333361451095805)
XLA Ops:
  0.6 0.8 dynamic_slice.6
  1.4 0.6 maximum_bitcast_fusion.freqs
  2.0 1.3 broadcast_in_dim.53.gamma
  3.3 0.7 iota_compare_fusion
  4.0 1.4 reshape.83.lens
  5.4 0.0 copy-start.1
  5.4 0.0 copy-start.2
  5.4 114.2 %project.1 = (bf16[384,1536]{1,0:T(8,128)(2,1)}, bf16[16,24,384]{2,1,0:T(8,128)(2,1)}, bf16[2,48,128]{2,1,0:T(8,128)(2,1)}) custom-call(bf16[2,8,4,48,768]{4,3,2,1,0:T(8,128)(2,1)} %bitcast.27, bf16[16,4,48,768]{3,2,1,0:T(8,128)(2,1)} %bitcast.28, bf16[768,384]{1,0:T(8,128)(2,1)} %wq.1, bf16[768,128]{1,0:T(8,128)(2,1)} %wk.1, bf16[768,128]{1,0:T(8,128)(2,1)} %wv.1, ...), custom_call_target="tpu_custom_call" | custom-call | tf_op jit(solution)/shard_map/project/pallas_call | solution.py:345
  119.6 0.7 dynamic-slice_bitcast_fusion
  120.3 1.3 reshape.84
  121.6 0.0 copy-done.1
  121.6 0.0 copy-done.2
  121.6 1.3 broadcast_select_fusion
  122.9 0.0 copy-start
  122.9 0.0 copy-start.3
  122.9 1.4 fusion.3
  124.3 0.4 fusion.11
  124.7 2.0 fusion.5
  126.8 0.0 copy-done
  126.8 0.0 copy-done.3
  126.8 0.2 copy.18
  126.9 1.0 reshape.85.att_in
  127.9 102.1 %combine.1 = bf16[2,8,4,2,24,768]{5,4,3,2,1,0:T(8,128)(2,1)} custom-call(bf16[16,24,384]{2,1,0:T(8,128)(2,1)} %reshape.85.att_in, bf16[4,2,48,1536]{3,2,1,0:T(8,128)(2,1)} %bitcast.31, bf16[2,8,4,2,24,768]{5,4,3,2,1,0:T(8,128)(2,1)} %bitcast.29, bf16[384,768]{1,0:T(8,128)(2,1)} %wo.1, bf16[1536,768]{1,0:T(8,128)(2,1)} %wd.1), custom_call_target="tpu_custom_call" | custom-call | tf_op jit(solution)/shard_map/combine/pallas_call | solution.py:727
  230.0 4.8 %copy.24 = bf16[3072,768]{1,0:T(8,128)(2,1)} copy(bf16[3072,768]{1,0:T(8,128)(2,1)} %bitcast.30) | data formatting | bytes 9437184
  (1 shorter events, 0.0 us)
Async XLA Ops:
  5.4 116.2 %copy-start.1 = (bf16[24,128,128]{2,1,0:T(8,128)(2,1)S(1)}, bf16[24,128,128]{2,1,0:T(8,128)(2,1)}, u32[]{:S(2)}) copy-start(bf16[24,128,128]{2,1,0:T(8,128)(2,1)} %param.14) | copy-start | bytes 2359300
  5.4 116.2 %copy-start.2 = (bf16[24,128,128]{2,1,0:T(8,128)(2,1)S(1)}, bf16[24,128,128]{2,1,0:T(8,128)(2,1)}, u32[]{:S(2)}) copy-start(bf16[24,128,128]{2,1,0:T(8,128)(2,1)} %param.15) | copy-start | bytes 2359300
  122.9 3.9 %copy-start = (bf16[24,128,128]{2,1,0:T(8,128)(2,1)}, bf16[24,128,128]{2,1,0:T(8,128)(2,1)S(1)}, u32[]{:S(2)}) copy-start(bf16[24,128,128]{2,1,0:T(8,128)(2,1)S(1)} %get-tuple-element.19) | copy-start | bytes 2359300
  122.9 3.9 %copy-start.3 = (bf16[24,128,128]{2,1,0:T(8,128)(2,1)}, bf16[24,128,128]{2,1,0:T(8,128)(2,1)S(1)}, u32[]{:S(2)}) copy-start(bf16[24,128,128]{2,1,0:T(8,128)(2,1)S(1)} %get-tuple-element.20) | copy-start | bytes 2359300

commit v4 on v3

--- a/solution.py
+++ b/solution.py
@@ -14,10 +14,16 @@
 CORES = 2
 TWO = 2
 LANES = 128
+TILE = 512
 BOTH = (0, 1)
 KINDS = (0, 1, 2)
 MIB = 2**20
-ORDER = "2030400250216003317041802251902332611033427143" + "528153629163721173828392931213"
+SIZES = (1, 2, 2, 2, 1)
+ORDER = (
+    "m1A0m0g1a0a1g0h0a2h1m2h2m3202130g2314041a3a451g35022h3616032"
+    + "m42371g4h4423381522443903462539144637254738283649293t194t0t3"
+    + "t2t4"
+)
 F32 = jnp.float32
 BF16 = jnp.bfloat16
 
@@ -67,7 +73,7 @@
     for d in range(RING):
         pieces.append((lambda c, d=d: x_main.at[c, :, d], xs.at[pl.ds(d * half_ty, half_ty), :, lanes]))
     pieces.append((lambda c: x_kv.at[row_idx], xs.at[pl.ds(RING * half_ty, RING), :, lanes]))
-    pieces.append((lambda c: gamma, gam.at[:, lanes]))
+    pieces.append((lambda c: gamma, gam.at[core]))
     pieces.append((lambda c: wq, ws.at[0, krows, pl.ds(0, q_width)]))
     kv_piece = len(pieces)
     pieces.append((lambda c: wk, wkvs.at[krows]))
@@ -104,7 +110,7 @@
 
     blk = 2 * group
     blocks = (RING * half_ty + RING) // 2
-    lane_tiles = kdim // 128
+    lane_tiles, slab_tiles = kdim // LANES, kblk // LANES
 
     def add_stats(slab):
         def stat_block(b, _):
@@ -146,7 +152,7 @@
         for j in range(lane_tiles):
             cols = slice(j * 128, (j + 1) * LANES)
             part = xs[pl.ds(2 * b, 2), :, cols].reshape(blk, LANES).astype(F32)
-            normed = ((part - mean_b) * rstd_b * gam[0:1, cols]).astype(BF16)
+            normed = ((part - mean_b) * rstd_b * gam[j // slab_tiles, pl.ds(j % slab_tiles, 1), :]).astype(BF16)
             xs[pl.ds(2 * b, 2), :, cols] = normed.reshape(2, group, LANES)
         return 0
 
@@ -355,7 +361,7 @@
             pltpu.VMEM((RING * half_ty + RING, group, kdim), BF16),
             pltpu.VMEM((steps + 1, kdim, wide), BF16),
             pltpu.VMEM((kdim, kv_width), BF16),
-            pltpu.VMEM((1, kdim), F32),
+            pltpu.VMEM((CORES, kblk // LANES, LANES), F32),
             pltpu.VMEM((stat_lines, LANES), F32),
             pltpu.VMEM((3, stat_lines, LANES), F32),
             pltpu.VMEM((steps + 1, rows, wide), BF16),
@@ -388,16 +394,16 @@
         ),
         name="project",
     )(
-        x_main, x_kv, wq, wk, wv, wg, wu, gamma_blk[None, :], lens.reshape(-1, group), inverse_freqs(head_dim)
+        x_main, x_kv, wq, wk, wv, wg, wu, gamma_blk.reshape(-1, LANES), lens.reshape(-1, group), inverse_freqs(head_dim)
     )
 
 
 def combine_kernel(
-    ty_size, chunks,
-    att_in, act_in, x_in, wo, wd,
+    ty_size,
+    q_in, k_in, v_in, act_in, x_in, wo, wd, lens,
     y_out,
-    att, mlp, wos, wds, yp, t1, xr, yf, p2_1, sd_1, sb_1, ra_1, rb_1, p2_2, sd_2, sb_2, ra_2, rb_2,
-    w_sem, wp_send, wp_recv, a2a_send, a2a_recv, mlp_sem, gx_send, gx_recv, x_sem, xp_send, xp_recv,
+    kc, vc, q_raw, q_f32, o_f32, att_out, att, mlp, wos, wds, yp, t1, xr, yf, p2_1, sd_1, sb_1, ra_1, rb_1, p2_2, sd_2, sb_2, ra_2, rb_2, ex,
+    qkv_sem, w_sem, wp_send, wp_recv, a2a_send, a2a_recv, mlp_sem, gx_send, gx_recv, x_sem, xp_send, xp_recv,
     rs_send, rs_recv, ag_send, ag_recv, out_sem, outp_send, outp_recv,
 ):
     row_idx = lax.axis_index("ty")
@@ -405,7 +411,10 @@
     ring_pos, core = col_idx // 2, col_idx % 2
     other = 1 - core
     half_ty = ty_size // 2
-    seq_block = att_in.shape[1]
+    chunks = len(SIZES)
+    begin = [sum(SIZES[:r]) for r in range(chunks)]
+    seq_block = q_in.shape[1]
+    group = 2 * seq_block
     cols = wo.shape[1]
     hcols = cols // 2
     pos_p, pos_m = (ring_pos + 1) % RING, (ring_pos + RING - 1) % RING
@@ -419,23 +428,41 @@
     z_side = (up(z_pos) * RING + y_pos, down(z_pos) * RING + y_pos)
     places = ((y_pos, z_pos), (z_pos, y_pos))
     sides = ((y_side, z_side), (z_side, y_side))
-    blk = yp.shape[1] // RING
-    sub = blk // RING
+    exchange = [size == 1 for size in SIZES]
     mine = pl.ds(pl.multiple_of(core * cols, LANES), cols)
+
+    def units(r):
+        return pl.ds(begin[r] * 2 * RING, SIZES[r] * 2 * RING)
+
+    def block_units(r, b):
+        return pl.ds(begin[r] * 2 * RING + b * 2 * SIZES[r], 2 * SIZES[r])
+
+    def unit(r, b1, b2):
+        return begin[r] * 2 * RING + b1 * 2 * SIZES[r] + b2
 
     def x_tile(c, r):
         b1, b2 = jnp.where(core == 0, y_pos, z_pos), jnp.where(core == 0, z_pos, y_pos)
-        return x_in.at[c, 2 * r + b2 // 2, b1, b2 % 2]
+        return x_in.at[c, block_units(r, b1) if exchange[r] else pl.ds(unit(r, b1, b2), 1)]
+
+    def x_slot(c, r):
+        return xr.at[c, r, pl.ds(0, 2 * SIZES[r] if exchange[r] else 1)]
+
+    def own(r):
+        return pl.ds(begin[r], SIZES[r])
 
     w_loads = [pltpu.make_async_copy(wd, wds.at[:, mine], w_sem.at[0]), pltpu.make_async_copy(wo, wos.at[:, mine], w_sem.at[1])]
     w_swaps = [
         remote(wd, wds.at[:, mine], wp_send.at[0], wp_recv.at[0], row_idx, tx_pair),
         remote(wo, wos.at[:, mine], wp_send.at[1], wp_recv.at[1], row_idx, tx_pair),
     ]
-    mlp_loads = [pltpu.make_async_copy(act_in.at[r], mlp.at[r, ring_pos], mlp_sem.at[r]) for r in range(chunks)]
-    x_loads = [pltpu.make_async_copy(x_tile(core, r), xr.at[core, r], x_sem.at[r]) for r in range(chunks)]
-    x_swaps = [remote(x_tile(other, r), xr.at[core, r], xp_send.at[r], xp_recv.at[r], row_idx, tx_pair) for r in range(chunks)]
-    for load in w_loads + mlp_loads + x_loads:
+    mlp_loads = [pltpu.make_async_copy(act_in.at[own(r)], mlp.at[own(r), ring_pos], mlp_sem.at[r]) for r in range(chunks)]
+    x_loads = [pltpu.make_async_copy(x_tile(core, r), x_slot(core, r), x_sem.at[r]) for r in range(chunks)]
+    x_swaps = [remote(x_tile(other, r), x_slot(core, r), xp_send.at[r], xp_recv.at[r], row_idx, tx_pair) for r in range(chunks)]
+    qkv_loads = [
+        pltpu.make_async_copy(src, dst, qkv_sem.at[n])
+        for n, (src, dst) in enumerate(((q_in, q_raw), (k_in, kc), (v_in, vc)))
+    ]
+    for load in qkv_loads + w_loads + mlp_loads + x_loads:
         load.start()
 
     barrier = pltpu.get_barrier_semaphore()
@@ -453,42 +480,74 @@
         sems = gx_send.at[r, part, stage, side], gx_recv.at[r, part, stage, side]
         buf = (mlp, att)[part]
         if stage == 0:
-            src = act_in.at[r] if part == 0 else att.at[r, ring_pos]
-            return remote(src, buf.at[r, ring_pos], *sems, row_idx, tx_side[side])
-        block = buf.at[r, from_side[side], side]
+            src = act_in.at[own(r)] if part == 0 else att.at[own(r), ring_pos]
+            return remote(src, buf.at[own(r), ring_pos], *sems, row_idx, tx_side[side])
+        if part == 0:
+            lanes = mlp.shape[-1] // 2
+            block = mlp.at[own(r), from_side[side], :, pl.ds(side * lanes, lanes)]
+        else:
+            block = att.at[own(r), from_side[side], side]
         return remote(block, block, *sems, row_idx, tx_side[side])
 
     home, home_core = row_idx % half_ty, row_idx // half_ty
 
     def a2a(k):
         return remote(
-            att_in.at[k], att.at[home // 2, ring_pos, home % 2, core], a2a_send.at[k], a2a_recv.at[home, core],
+            att_out.at[k], att.at[home, ring_pos, core], a2a_send.at[k], a2a_recv.at[home, core],
             k, ring_pos * 2 + home_core,
         )
 
     def a2a_self(k):
         return jnp.logical_and(k == row_idx, core == home_core)
 
-    for side in BOTH:
-        gather(0, 0, 0, side).start()
-    for k in range(ty_size):
-        @pl.when(a2a_self(k))
-        def _():
-            pltpu.make_async_copy(
-                att_in.at[k], att.at[home // 2, ring_pos, home % 2, core], a2a_recv.at[home, core]
-            ).start()
-
-        @pl.when(jnp.logical_not(a2a_self(k)))
-        def _():
-            a2a(k).start()
+    def attend(_):
+        heads, lines, head_dim = q_f32.shape
+        for load in qkv_loads:
+            load.wait()
+        for k in range(ty_size):
+            for h in range(heads):
+                lanes = slice(h * head_dim, (h + 1) * head_dim)
+                q_f32[h, k * seq_block : (k + 1) * seq_block, :] = q_raw[k, :, lanes].astype(F32)
+        slots = lax.broadcasted_iota(jnp.int32, (heads * ty_size, kc.shape[1]), 1)
+
+        def sequence(b, _):
+            picked = pl.ds(b, ty_size, stride=seq_block)
+            queries = jnp.concatenate([q_f32[h, picked, :] for h in range(heads)]).astype(BF16)
+            scores = lax.dot_general(
+                queries, kc[b], (((1,), (1,)), ((), ())), preferred_element_type=F32
+            ) * (head_dim**-0.5)
+            scores = jnp.where(slots <= lens[b], scores, -1e30)
+            weights = jnp.exp(scores - jnp.max(scores, axis=1, keepdims=True))
+            probs = (weights / jnp.sum(weights, axis=1, keepdims=True)).astype(BF16)
+            mixed = jnp.dot(probs, vc[b], preferred_element_type=F32)
+            for h in range(heads):
+                o_f32[h, picked, :] = mixed[h * ty_size : (h + 1) * ty_size]
+            return 0
+
+        lax.fori_loop(0, seq_block, sequence, 0, unroll=8)
+        for k in range(ty_size):
+            for h in range(heads):
+                lanes = slice(h * head_dim, (h + 1) * head_dim)
+                att_out[k, :, lanes] = o_f32[h, k * seq_block : (k + 1) * seq_block, :].astype(BF16)
+        for k in range(ty_size):
+            @pl.when(a2a_self(k))
+            def _():
+                pltpu.make_async_copy(
+                    att_out.at[k], att.at[home, ring_pos, core], a2a_recv.at[home, core]
+                ).start()
+
+            @pl.when(jnp.logical_not(a2a_self(k)))
+            def _():
+                a2a(k).start()
+
     for swap in w_swaps + x_swaps:
         swap.start()
 
     def att_ready(r):
-        for g in (2 * r, 2 * r + 1):
+        for g in range(begin[r], begin[r] + SIZES[r]):
             for cc in BOTH:
                 remote(
-                    att_in.at[0], att.at[r, ring_pos, g % 2, cc], a2a_send.at[0], a2a_recv.at[g, cc], row_idx, tx_pair
+                    att_out.at[0], att.at[g, ring_pos, cc], a2a_send.at[0], a2a_recv.at[g, cc], row_idx, tx_pair
                 ).wait_recv()
 
     def own_att(r):
@@ -500,38 +559,41 @@
         for side in BOTH:
             gather(r, 0, 0, side).start()
 
-    def forward(r):
-        for part in BOTH:
-            for side in BOTH:
-                gather(r, part, 0, side).wait_recv()
-                gather(r, part, 1, side).start()
+    def forward(part, r):
+        for side in BOTH:
+            gather(r, part, 0, side).wait_recv()
+            gather(r, part, 1, side).start()
 
     def multiply(r):
         mlp_loads[r].wait()
         for part in BOTH:
             for side in BOTH:
                 gather(r, part, 1, side).wait_recv()
-        rows = yp.shape[1]
+        rows = SIZES[r] * RING * group
 
         def tile(n, _):
-            lanes = pl.ds(pl.multiple_of(n * 512, 512), 512)
-            left_mlp = mlp[r].reshape(rows, mlp.shape[-1])
-            left_att = att[r].reshape(rows, att.shape[-1])
-            yp[r, :, lanes] = jnp.dot(left_mlp, wds[:, lanes], preferred_element_type=F32) + jnp.dot(
-                left_att, wos[:, lanes], preferred_element_type=F32
-            )
+            lanes = pl.ds(pl.multiple_of(n * TILE, TILE), TILE)
+            left_mlp = mlp[own(r)].reshape(rows, mlp.shape[-1])
+            left_att = att[own(r)].reshape(rows, att.shape[-1])
+            yp[pl.ds(begin[r] * RING * group, rows), lanes] = jnp.dot(
+                left_mlp, wds[:, lanes], preferred_element_type=F32
+            ) + jnp.dot(left_att, wos[:, lanes], preferred_element_type=F32)
             return 0
 
-        lax.fori_loop(0, yp.shape[2] // 512, tile, 0)
+        lax.fori_loop(0, yp.shape[1] // TILE, tile, 0)
 
     bufs = ((p2_1, sd_1, sb_1, ra_1, rb_1), (p2_2, sd_2, sb_2, ra_2, rb_2))
+
+    def block_rows(level, r):
+        return (SIZES[r] * group, seq_block)[level]
 
     def hop(level, r, c, kind, side):
         p2, sd, sb, ra, rb = bufs[level]
+        m = pl.ds(0, block_rows(level, r))
         src, dst = (
-            (p2.at[r, c, :, pl.ds(side * hcols, hcols)], ra.at[r, c, side]),
-            (sd.at[r, c, side], rb.at[r, c, side, 0]),
-            (sb.at[r, c, side], rb.at[r, c, side, 1]),
+            (p2.at[r, c, m, pl.ds(side * hcols, hcols)], ra.at[r, c, side, m]),
+            (sd.at[r, c, side, m], rb.at[r, c, side, 0, m]),
+            (sb.at[r, c, side, m], rb.at[r, c, side, 1, m]),
         )[kind]
         return remote(
             src, dst, rs_send.at[level, r, c, kind, side], rs_recv.at[level, r, c, kind, side],
@@ -539,37 +601,39 @@
         )
 
     def part_of(level, r, c, b, half):
-        size = (blk, sub)[level]
-        rows = pl.ds(pl.multiple_of(b * size, 8), size)
+        size = block_rows(level, r)
         if level == 0:
-            return yp[r, rows, c * cols + half * hcols : c * cols + (half + 1) * hcols]
-        return t1[r, c, rows, half * hcols : (half + 1) * hcols]
+            rows = pl.ds(pl.multiple_of(begin[r] * RING * group + b * size, 8), size)
+            return yp[rows, c * cols + half * hcols : c * cols + (half + 1) * hcols]
+        return t1[r, c, pl.ds(pl.multiple_of(b * size, 8), size), half * hcols : (half + 1) * hcols]
 
     def reduce_a(level, r):
         p2, sd = bufs[level][:2]
+        m = block_rows(level, r)
         for c in BOTH:
             pos = places[c][level]
             for half in BOTH:
-                p2[r, c, :, half * hcols : (half + 1) * hcols] = part_of(level, r, c, (pos + 2) % RING, half).astype(BF16)
+                p2[r, c, :m, half * hcols : (half + 1) * hcols] = part_of(level, r, c, (pos + 2) % RING, half).astype(BF16)
                 hop(level, r, c, 0, half).start()
         for c in BOTH:
             pos = places[c][level]
-            sd[r, c, 0] = part_of(level, r, c, up(pos), 1).astype(BF16)
-            hop(level, r, c, 1, 0).start()
-            sd[r, c, 1] = part_of(level, r, c, down(pos), 0).astype(BF16)
-            hop(level, r, c, 1, 1).start()
+            for side, b in enumerate((up(pos), down(pos))):
+                sd[r, c, side, :m] = part_of(level, r, c, b, 1 - side).astype(BF16)
+                hop(level, r, c, 1, side).start()
 
     def reduce_b(level, r):
         sb, ra = bufs[level][2:4]
+        m = block_rows(level, r)
         for c in BOTH:
             pos = places[c][level]
-            for side, b in ((0, up(pos)), (1, down(pos))):
+            for side, b in enumerate((up(pos), down(pos))):
                 hop(level, r, c, 0, side).wait_recv()
-                sb[r, c, side] = (part_of(level, r, c, b, side) + ra[r, c, side].astype(F32)).astype(BF16)
+                sb[r, c, side, :m] = (part_of(level, r, c, b, side) + ra[r, c, side, :m].astype(F32)).astype(BF16)
                 hop(level, r, c, 2, side).start()
 
     def reduce_c(level, r, finish):
         rb = bufs[level][4]
+        m = block_rows(level, r)
         for c in BOTH:
             pos = places[c][level]
             for half in BOTH:
@@ -577,22 +641,24 @@
                 hop(level, r, c, 2, half).wait_recv()
                 finish(
                     c, half,
-                    part_of(level, r, c, pos, half) + rb[r, c, half, 1].astype(F32) + rb[r, c, 1 - half, 0].astype(F32),
+                    part_of(level, r, c, pos, half)
+                    + rb[r, c, half, 1, :m].astype(F32) + rb[r, c, 1 - half, 0, :m].astype(F32),
                 )
 
     def spread(level, r, c, stage, side):
         ring, (p1, p2) = sides[c][level], places[c]
         sems = ag_send.at[level, r, c, stage, side], ag_recv.at[level, r, c, stage, side]
         near = (down, up)[side]
-        if level == 1:
-            if stage == 0:
-                block = yf.at[r, c, p1, p2 // 2, p2 % 2]
-            else:
-                block = yf.at[r, c, p1, near(p2) // 2, near(p2) % 2, :, pl.ds(side * hcols, hcols)]
+        half = pl.ds(side * hcols, hcols)
+        if level == 1 and exchange[r]:
+            m = pl.ds(0, block_rows(0, r))
+            block = ex.at[r, c, p2, m] if stage == 0 else ex.at[r, c, near(p2), m, half]
+        elif level == 1:
+            block = yf.at[c, unit(r, p1, p2)] if stage == 0 else yf.at[c, unit(r, p1, near(p2)), :, half]
         elif stage == 0:
-            block = yf.at[r, c, p1]
+            block = yf.at[c, block_units(r, p1)]
         else:
-            block = yf.at[r, c, near(p1), side]
+            block = yf.at[c, pl.ds(unit(r, near(p1), side * SIZES[r]), SIZES[r])]
         return remote(block, block, *sems, ring[side], col_idx)
 
     def spread_own(level, r):
@@ -615,24 +681,45 @@
         reduce_b(0, r)
 
     def s4(r):
+        m = block_rows(0, r)
+
         def finish(c, half, vals):
-            t1[r, c, :, half * hcols : (half + 1) * hcols] = vals
+            lanes = slice(half * hcols, (half + 1) * hcols)
+            if exchange[r]:
+                ex[r, c, places[c][1], :m, lanes] = vals.astype(BF16)
+            else:
+                t1[r, c, :m, lanes] = vals
         reduce_c(0, r, finish)
-        reduce_a(1, r)
+        if exchange[r]:
+            spread_own(1, r)
+        else:
+            reduce_a(1, r)
 
     def s5(r):
-        reduce_b(1, r)
+        if exchange[r]:
+            spread_on(1, r)
+        else:
+            reduce_b(1, r)
 
     def s6(r):
         x_loads[r].wait()
-        remote(x_tile(other, r), xr.at[other, r], xp_send.at[r], xp_recv.at[r], row_idx, tx_pair).wait_recv()
-
-        def finish(c, half, vals):
-            lanes = slice(half * hcols, (half + 1) * hcols)
-            p1, p2 = places[c]
-            yf[r, c, p1, p2 // 2, p2 % 2, :, lanes] = (xr[c, r, :, lanes].astype(F32) + vals).astype(BF16)
-        reduce_c(1, r, finish)
-        spread_own(1, r)
+        remote(x_tile(other, r), x_slot(other, r), xp_send.at[r], xp_recv.at[r], row_idx, tx_pair).wait_recv()
+        if exchange[r]:
+            m = block_rows(0, r)
+            spread_end(1, r)
+            for c in BOTH:
+                for n in range(2 * SIZES[r]):
+                    rows = slice(n * seq_block, (n + 1) * seq_block)
+                    first, second, third, fourth = (ex[r, c, p, rows].astype(F32) for p in range(RING))
+                    total = (first + second) + (third + fourth)
+                    yf[c, unit(r, places[c][0], n)] = (xr[c, r, n].astype(F32) + total).astype(BF16)
+            spread_own(0, r)
+        else:
+            def finish(c, half, vals):
+                lanes = slice(half * hcols, (half + 1) * hcols)
+                yf[c, unit(r, *places[c]), :, lanes] = (xr[c, r, 0, :, lanes].astype(F32) + vals).astype(BF16)
+            reduce_c(1, r, finish)
+            spread_own(1, r)
 
     def s7(r):
         spread_on(1, r)
@@ -644,42 +731,34 @@
     def s9(r):
         spread_on(0, r)
 
-    def out_copy(r, p):
-        return pltpu.make_async_copy(
-            yf.at[r, core, p], y_out.at[core, pl.ds(2 * r, 2), p], out_sem.at[r, p]
-        )
-
-    def out_swap(r, p):
+    def out_copy(r):
+        return pltpu.make_async_copy(yf.at[core, units(r)], y_out.at[core, units(r)], out_sem.at[r])
+
+    def out_swap(r):
         return remote(
-            yf.at[r, other, p], y_out.at[core, pl.ds(2 * r, 2), p],
-            outp_send.at[r, p], outp_recv.at[r, p], row_idx, tx_pair,
+            yf.at[other, units(r)], y_out.at[core, units(r)], outp_send.at[r], outp_recv.at[r], row_idx, tx_pair
         )
 
     def s10(r):
         spread_end(0, r)
-        for p in range(RING):
-            out_swap(r, p).start()
-            out_copy(r, p).start()
+        out_swap(r).start()
+        out_copy(r).start()
 
     def s2(r):
         multiply(r)
         reduce_a(0, r)
 
-    own_mlp(1)
-    own_att(0)
-    own_att(1)
-    forward(0)
-    own_mlp(2)
-    own_att(2)
-    forward(1)
-    own_mlp(3)
-    own_att(3)
-    for n in BOTH:
-        w_loads[n].wait()
-        w_swaps[n].wait_recv()
-    stages = (forward, s10, s2, s3, s4, s5, s6, s7, s8, s9)
-    for stage, r in zip(ORDER[0::TWO], ORDER[1::TWO]):
-        stages[int(stage)](int(r))
+    stages = dict(zip("mAagh23456789t", (
+        own_mlp, attend, own_att, functools.partial(forward, 0), functools.partial(forward, 1),
+        s2, s3, s4, s5, s6, s7, s8, s9, s10,
+    )))
+    products = ORDER[::TWO].index("2") * TWO
+    for n in range(0, len(ORDER), TWO):
+        if n == products:
+            for load, swap in zip(w_loads, w_swaps):
+                load.wait()
+                swap.wait_recv()
+        stages[ORDER[n]](int(ORDER[n + 1]))
 
     for swap in w_swaps + x_swaps:
         swap.wait_send()
@@ -694,71 +773,67 @@
                     gather(r, a, b, side).wait_send()
                     for level in BOTH:
                         spread(level, r, a, b, side).wait_send()
-        for level in BOTH:
+        for level in BOTH[: 2 - exchange[r]]:
             for c in BOTH:
                 for kind in KINDS:
                     for side in BOTH:
                         hop(level, r, c, kind, side).wait_send()
-        for p in range(RING):
-            out_copy(r, p).wait()
-            out_swap(r, p).wait()
-
-
-def combine(att_owned, act_own, x_blk, w_out, w_down, ty_size):
-    seq_block = att_owned.shape[1]
-    chunks = ty_size // 4
-    group, half_ty = 2 * seq_block, ty_size // 2
+        out_copy(r).wait()
+        out_swap(r).wait()
+
+
+def combine(q_owned, k_out, v_out, lens_own, act_own, x_blk, w_out, w_down, ty_size):
+    seq_block = q_owned.shape[1]
+    head_dim = k_out.shape[TWO]
+    chunks, most = len(SIZES), max(SIZES)
+    group, half_ty = TWO * seq_block, ty_size // TWO
     cols = w_out.shape[1]
-    per = half_ty // chunks
+    hcols = cols // TWO
     ffn, q_width = w_down.shape[0], w_out.shape[0]
-    crows = RING * per * group
-    blk, sub, hcols = crows // RING, crows // RING // RING, cols // 2
     any_spec = pl.BlockSpec(memory_space=pl.ANY)
     ring_bufs = []
-    for m in (blk, sub):
-        ring_bufs += [
-            pltpu.VMEM((chunks, TWO, m, cols), BF16),
-            pltpu.VMEM((chunks, TWO, TWO, m, hcols), BF16),
-            pltpu.VMEM((chunks, TWO, TWO, m, hcols), BF16),
-            pltpu.VMEM((chunks, TWO, TWO, m, hcols), BF16),
-            pltpu.VMEM((chunks, TWO, TWO, TWO, m, hcols), BF16),
-        ]
+    for m in (most * group, seq_block):
+        half = (chunks, TWO, TWO, m, hcols)
+        both = (chunks, TWO, TWO, TWO, m, hcols)
+        ring_bufs += [pltpu.VMEM(shape, BF16) for shape in ((chunks, TWO, m, cols), half, half, half, both)]
     dma = pltpu.SemaphoreType.DMA
+    y_units = (TWO, half_ty * RING * TWO, seq_block, cols)
     y = pl.pallas_call(
-        functools.partial(combine_kernel, ty_size, chunks),
-        out_shape=jax.ShapeDtypeStruct((TWO, half_ty, RING, TWO, seq_block, cols), BF16),
-        in_specs=[any_spec] * 5,
+        functools.partial(combine_kernel, ty_size),
+        out_shape=jax.ShapeDtypeStruct(y_units, BF16),
+        in_specs=[any_spec] * 7 + [pl.BlockSpec(memory_space=pltpu.SMEM)],
         out_specs=any_spec,
         scratch_shapes=[
-            pltpu.VMEM((chunks, RING, per, TWO, seq_block, q_width), BF16),
-            pltpu.VMEM((chunks, RING, per, group, ffn), BF16),
+            pltpu.VMEM(k_out.shape, BF16),
+            pltpu.VMEM(v_out.shape, BF16),
+            pltpu.VMEM(q_owned.shape, BF16),
+            pltpu.VMEM((q_width // head_dim, ty_size * seq_block, head_dim), F32),
+            pltpu.VMEM((q_width // head_dim, ty_size * seq_block, head_dim), F32),
+            pltpu.VMEM(q_owned.shape, BF16),
+            pltpu.VMEM((half_ty, RING, TWO, seq_block, q_width), BF16),
+            pltpu.VMEM((half_ty, RING, group, ffn), BF16),
             pltpu.VMEM((q_width, TWO * cols), BF16),
             pltpu.VMEM((ffn, TWO * cols), BF16),
-            pltpu.VMEM((chunks, crows, TWO * cols), F32),
-            pltpu.VMEM((chunks, TWO, blk, cols), F32),
-            pltpu.VMEM((TWO, chunks, seq_block, cols), BF16),
-            pltpu.VMEM((chunks, TWO, RING, TWO, TWO, seq_block, cols), BF16),
+            pltpu.VMEM((half_ty * RING * group, TWO * cols), F32),
+            pltpu.VMEM((chunks, TWO, most * group, cols), F32),
+            pltpu.VMEM((TWO, chunks, TWO * most, seq_block, cols), BF16),
+            pltpu.VMEM(y_units, BF16),
             *ring_bufs,
-            dma((CORES,)), dma((CORES,)), dma((CORES,)),
+            pltpu.VMEM((chunks, TWO, RING, most * group, cols), BF16),
+            dma((len(KINDS),)), dma((CORES,)), dma((CORES,)), dma((CORES,)),
             dma((ty_size,)), dma((half_ty, TWO)),
             dma((chunks,)),
             dma((chunks, TWO, TWO, TWO)), dma((chunks, TWO, TWO, TWO)),
             dma((chunks,)), dma((chunks,)), dma((chunks,)),
             dma((TWO, chunks, TWO, len(KINDS), TWO)), dma((TWO, chunks, TWO, len(KINDS), TWO)),
             dma((TWO, chunks, TWO, TWO, TWO)), dma((TWO, chunks, TWO, TWO, TWO)),
-            dma((chunks, RING)), dma((chunks, RING)), dma((chunks, RING)),
+            dma((chunks,)), dma((chunks,)), dma((chunks,)),
         ],
         compiler_params=pltpu.CompilerParams(
             collective_id=1, has_side_effects=True, vmem_limit_bytes=60 * MIB
         ),
         name="combine",
-    )(
-        att_owned,
-        act_own.reshape(chunks, per, group, ffn),
-        x_blk.reshape(TWO, half_ty, RING, TWO, seq_block, cols),
-        w_out,
-        w_down,
-    )
+    )(q_owned, k_out, v_out, act_own.reshape(half_ty, group, ffn), x_blk.reshape(y_units), w_out, w_down, lens_own)
     return y.reshape(x_blk.shape)
 
 
@@ -771,7 +846,6 @@
         rows = x_blk.shape[0]
         d_model = x_blk.shape[1] * tx_size
         seq_block, ctx_len, head_dim = k_blk.shape
-        local_heads = w_query.shape[1] // head_dim
         row_idx = lax.axis_index("ty")
         col_idx = lax.axis_index("tx")
         ring_pos, core = col_idx // 2, col_idx % 2
@@ -789,14 +863,7 @@
         k_out = jnp.where(at_slot, kv_own[0][:, None, :], k_blk)
         v_out = jnp.where(at_slot, kv_own[1][:, None, :], v_blk)
 
-        q_owned = q_owned.reshape(ty_size, seq_block, local_heads, head_dim)
-        scores = jnp.einsum("gbhd,btd->gbht", q_owned, k_out, preferred_element_type=F32) * (head_dim ** -0.5)
-        in_range = positions[None, None, None, :] <= lens_own[None, :, None, None]
-        scores = jnp.where(in_range, scores, -1e30)
-        att_probs = jax.nn.softmax(scores, axis=-1).astype(BF16)
-        att_owned = jnp.einsum("gbht,btd->gbhd", att_probs, v_out, preferred_element_type=F32).astype(BF16)
-        att_owned = att_owned.reshape(ty_size, seq_block, local_heads * head_dim)
-        y_blk = combine(att_owned, act_own, x_blk, w_out, w_down, ty_size)
+        y_blk = combine(q_owned, k_out, v_out, lens_own, act_own, x_blk, w_out, w_down, ty_size)
         return y_blk, k_out, v_out
 
     in_specs = (P("dp", "tx"), P("dp"), cache_spec, cache_spec, P("tx"), P("tx", "ty"), P("tx", None), P("tx", None), P("tx", "ty"), P("tx", "ty"), P("ty", "tx"), P("ty", "tx"))

time: 235 us -> 225 us (0.957)
  local copies, waits for them, and re-layouts: 11.4 us -> 7.73 us
  matrix products: 3.41 us -> 0 us
    dot_general x2 -> x0, matrix products: 3.41 us -> none  [the longest x1 2.03 us: layer_shard(): jnp.einsum('gbht,btd->gbhd', att_probs, v_out, preferred_element_type=F32)]
    unnamed x9 -> x7, local copies, waits for them, and re-layouts: 4.85 us -> 4.84 us
where the time goes in v4:
time: 225 us
  Pallas kernels  214 us (95%)
  local copies, waits for them, and re-layouts  7.73 us (3%)
    pallas_call x1, Pallas kernels, project(): pl.pallas_call(functools.partial(project_kernel, ty_size, tile, d_model),...  114 us
    pallas_call x1, Pallas kernels, combine(): pl.pallas_call(functools.partial(combine_kernel, ty_size), out_shape=jax....  100 us
    unnamed x7, local copies, waits for them, and re-layouts  4.84 us

profile of v4, /device:TPU:1, one launch (start us, length us, event | category | flops | bytes accessed | tf_op | source)
XLA Modules:
  0.0 224.8 jit_solution(13639971533210970201)
XLA Ops:
  0.6 0.8 dynamic_slice.6.lens
  1.4 0.0 copy-start.2
  1.4 0.6 maximum_bitcast_fusion.freqs
  2.0 0.1 iota_compare_fusion
  2.1 1.4 reshape.57.lens
  3.5 0.0 copy-start
  3.5 0.0 copy-start.1
  3.5 114.2 %project.1 = (bf16[384,1536]{1,0:T(8,128)(2,1)}, bf16[16,24,384]{2,1,0:T(8,128)(2,1)}, bf16[2,48,128]{2,1,0:T(8,128)(2,1)}) custom-call(bf16[2,8,4,48,768]{4,3,2,1,0:T(8,128)(2,1)} %bitcast.12, bf16[16,4,48,768]{3,2,1,0:T(8,128)(2,1)} %bitcast.13, bf16[768,384]{1,0:T(8,128)(2,1)} %wq.1, bf16[768,128]{1,0:T(8,128)(2,1)} %wk.1, bf16[768,128]{1,0:T(8,128)(2,1)} %wv.1, ...), custom_call_target="tpu_custom_call" | custom-call | tf_op jit(solution)/shard_map/project/pallas_call | solution.py:351
  117.7 0.0 copy-done.2
  117.7 0.7 dynamic-slice_bitcast_fusion
  118.4 0.0 copy-done
  118.4 0.0 copy-done.1
  118.5 1.5 broadcast_select_fusion
  119.9 100.1 %combine.1 = bf16[2,64,24,768]{3,2,1,0:T(8,128)(2,1)} custom-call(bf16[16,24,384]{2,1,0:T(8,128)(2,1)} %get-tuple-element.6.q_in, bf16[24,128,128]{2,1,0:T(8,128)(2,1)} %get-tuple-element.17.k_in, bf16[24,128,128]{2,1,0:T(8,128)(2,1)} %get-tuple-element.18.v_in, bf16[8,48,1536]{2,1,0:T(8,128)(2,1)} %bitcast.16, bf16[2,64,24,768]{3,2,1,0:T(8,128)(2,1)} %bitcast.14, ...), custom_call_target="tpu_custom_call" | custom-call | tf_op jit(solution)/shard_map/combine/pallas_call | solution.py:801
  220.0 4.8 %copy.16 = bf16[3072,768]{1,0:T(8,128)(2,1)} copy(bf16[3072,768]{1,0:T(8,128)(2,1)} %bitcast.15) | data formatting | bytes 9437184
  (1 shorter events, 0.0 us)
Async XLA Ops:
  1.4 116.3 %copy-start.2 = (s32[24]{0:T(128)}, s32[24]{0:T(128)S(1)}, u32[]{:S(2)}) copy-start(s32[24]{0:T(128)S(1)} %dynamic_slice.6.lens) | copy-start | bytes 292
  3.5 114.9 %copy-start = (bf16[24,128,128]{2,1,0:T(8,128)(2,1)S(1)}, bf16[24,128,128]{2,1,0:T(8,128)(2,1)}, u32[]{:S(2)}) copy-start(bf16[24,128,128]{2,1,0:T(8,128)(2,1)} %param.15) | copy-start | bytes 2359300
  3.5 114.9 %copy-start.1 = (bf16[24,128,128]{2,1,0:T(8,128)(2,1)S(1)}, bf16[24,128,128]{2,1,0:T(8,128)(2,1)}, u32[]{:S(2)}) copy-start(bf16[24,128,128]{2,1,0:T(8,128)(2,1)} %param.14) | copy-start | bytes 2359300

commit v5 on v4

--- a/solution.py
+++ b/solution.py
@@ -2,6 +2,7 @@
 
 import jax
 import jax.numpy as jnp
+import numpy as np
 from jax import lax
 from jax.experimental import pallas as pl
 from jax.experimental.pallas import tpu as pltpu
@@ -29,9 +30,14 @@
 
 
 def inverse_freqs(head_dim):
-    half_dim = head_dim // 2
-    freqs = ROPE_BASE ** (-(jnp.arange(half_dim, dtype=F32) * 2.0) / head_dim)
-    return jnp.concatenate([freqs, freqs])[None, :]
+    powers = np.arange(head_dim // 2, dtype=np.float32) * np.float32(2.0) / np.float32(head_dim)
+    freqs = np.float32(ROPE_BASE) ** -powers
+    return jnp.asarray(np.concatenate([freqs, freqs])[None, :])
+
+
+def updated(cache, row, length):
+    slots = lax.broadcasted_iota(jnp.int32, cache.shape, 0)
+    return jnp.where(slots == length, row, cache.astype(F32)).astype(BF16)
 
 
 def remote(src, dst, send_sem, recv_sem, ty, tx):
@@ -46,7 +52,7 @@
     x_main, x_kv, wq, wk, wv, wg, wu, gamma, lens, freqs,
     act_out, q_out, kv_out,
     xs, ws, wkvs, gam, st, sr, p2, sd, sb, ra, rb, act, kvs, kvr, kvf, qs, qr,
-    load_sem, pair_send, pair_recv, st_send, st_recv, ssem, rsem, kv_ssem, kv_rsem, kvf_sem, q_ssem, q_rsem, out_sem,
+    load_sem, pair_send, pair_recv, st_send, st_recv, ssem, rsem, kv_ssem, kv_rsem, kvf_sem, q_ssem, q_rsem, act_sem, out_sem,
 ):
     row_idx = lax.axis_index("ty")
     col_idx = lax.axis_index("tx")
@@ -82,15 +88,17 @@
         pieces.append((lambda c, t=t: wu.at[:, pl.ds(t * tile, tile)], ws.at[t + 1, krows, pl.ds(tile, tile)]))
     loads = [pltpu.make_async_copy(src(core), dst, load_sem.at[n]) for n, (src, dst) in enumerate(pieces)]
     swaps = [remote(src(other), dst, pair_send.at[n], pair_recv.at[n], row_idx, tx_pair) for n, (src, dst) in enumerate(pieces)]
-    def start(copies, kv_copies, wants):
+    def start(copies, kv_copies, wants, first):
         for n, copy in enumerate(copies):
+            if n < first:
+                continue
             if n != kv_piece:
                 copy.start()
             else:
                 for which in BOTH:
                     pl.when(wants == which)(kv_copies[which].start)
 
-    start(loads, [pltpu.make_async_copy(w, wkvs.at[krows], load_sem.at[kv_piece]) for w in (wk, wv)], core)
+    start(loads, [pltpu.make_async_copy(w, wkvs.at[krows], load_sem.at[kv_piece]) for w in (wk, wv)], core, 0)
     st[...] = jnp.zeros_like(st)
 
     barrier = pltpu.get_barrier_semaphore()
@@ -106,13 +114,15 @@
     kv_swaps = [
         remote(w, wkvs.at[krows], pair_send.at[kv_piece], pair_recv.at[kv_piece], row_idx, tx_pair) for w in (wk, wv)
     ]
-    start(swaps, kv_swaps, other)
+    for swap in swaps[: kv_piece - 1]:
+        swap.start()
 
     blk = 2 * group
     blocks = (RING * half_ty + RING) // 2
+    per_dest = half_ty // 2
     lane_tiles, slab_tiles = kdim // LANES, kblk // LANES
 
-    def add_stats(slab):
+    def add_stats(slab, first, count):
         def stat_block(b, _):
             def lane_tile(j, sums):
                 tile_lanes = pl.ds(pl.multiple_of(slab * kblk + j * LANES, LANES), LANES)
@@ -125,14 +135,16 @@
                 st[line, pl.ds(0, blk)] += jnp.sum(sums[which].T, axis=0, keepdims=True)
             return 0
 
-        lax.fori_loop(0, blocks, stat_block, 0)
+        lax.fori_loop(first, first + count, stat_block, 0)
 
     for n in range(kv_piece - 1):
         loads[n].wait()
-    add_stats(core)
+    add_stats(core, 0, blocks)
     for n in range(kv_piece - 1):
         swaps[n].wait_recv()
-    add_stats(other)
+        if n <= RING:
+            add_stats(other, n * per_dest, per_dest if n < RING else RING // 2)
+    start(swaps, kv_swaps, other, kv_piece - 1)
     stat_copies = [
         remote(st, sr.at[n], st_send.at[n], st_recv.at[n], row_idx, tx) for n, tx in enumerate((tx_p, tx_m, tx_o))
     ]
@@ -156,7 +168,6 @@
             xs[pl.ds(2 * b, 2), :, cols] = normed.reshape(2, group, LANES)
         return 0
 
-    per_dest = half_ty // 2
 
     def norm_dest(d, count):
         lax.fori_loop(d * per_dest, d * per_dest + count, norm_block, 0)
@@ -229,6 +240,10 @@
                 for k in BOTH:
                     qs[2 * (half * hg + g) + k, :, cols] = turned[k * seq_block : (k + 1) * seq_block]
 
+    def act_copy(s):
+        tile_lanes = pl.ds(pl.multiple_of((s - 1) * tile, tile), tile)
+        return pltpu.make_async_copy(act.at[:, tile_lanes], act_out.at[:, tile_lanes], act_sem.at[s])
+
     def finish_mlp(s):
         def finish(half, vals):
             gate = vals[:, :tile].astype(BF16).astype(F32)
@@ -236,6 +251,8 @@
             act[pl.ds(half * hrows, hrows), pl.ds(pl.multiple_of((s - 1) * tile, tile), tile)] = (
                 gate * jax.nn.sigmoid(gate) * up
             ).astype(BF16)
+            if half:
+                act_copy(s).start()
         return finish
 
     def q_copy(k):
@@ -264,9 +281,13 @@
     for n, pos in enumerate((pos_p, pos_m, pos_o)):
         kv_copy(n, pos).start()
     norm_dest(ring_pos, per_dest)
-    for n in range(kv_piece + 1, len(loads)):
-        loads[n].wait()
-        swaps[n].wait_recv()
+
+    def weights_here(first, last):
+        for n in range(kv_piece + 2 * first - 1, kv_piece + 2 * last + 1):
+            loads[n].wait()
+            swaps[n].wait_recv()
+
+    weights_here(1, 1)
     stage_a(1, wide)
     stage_b(0, q_width)
     for n, pos in enumerate((pos_p, pos_m, pos_o)):
@@ -275,6 +296,7 @@
     kvf[core] = turn(new_row, *tables(lens[pl.ds(row_idx * RING + ring_pos, 1), :] * other)).astype(BF16)
     kv_pair = remote(kvf.at[core], kvf.at[core], kvf_sem.at[0], kvf_sem.at[1], row_idx, tx_pair)
     kv_pair.start()
+    weights_here(2, 2)
     stage_a(2, wide)
     stage_b(1, wide)
     stage_c(0, q_width, finish_q)
@@ -293,23 +315,22 @@
         stage_c(s - 2, wide, finish_mlp(s - 2))
         return 0
 
+    weights_here(3, steps)
     lax.fori_loop(3, steps + 1, middle, 0)
     stage_b(steps, wide)
     stage_c(steps - 1, wide, finish_mlp(steps - 1))
     stage_c(steps, wide, finish_mlp(steps))
 
     outs = [
-        pltpu.make_async_copy(act, act_out, out_sem.at[0]),
-        pltpu.make_async_copy(qr, q_out, out_sem.at[1]),
-        pltpu.make_async_copy(kvf, kv_out, out_sem.at[2]),
+        pltpu.make_async_copy(qr, q_out, out_sem.at[0]),
+        pltpu.make_async_copy(kvf, kv_out, out_sem.at[1]),
     ]
-    outs[0].start()
     for k in range(ty_size):
         remote(qs.at[0], qr.at[k], q_ssem.at[0], q_rsem.at[k], row_idx, tx_pair).wait_recv()
-    outs[1].start()
+    outs[0].start()
     kv_pair.wait_send()
     remote(kvf.at[other], kvf.at[other], kvf_sem.at[0], kvf_sem.at[1], row_idx, tx_pair).wait_recv()
-    outs[2].start()
+    outs[1].start()
     for k in range(ty_size):
         @pl.when(jnp.logical_not(q_is_self(k)))
         def _():
@@ -323,6 +344,7 @@
             hop(0, q_width, kind, side).wait_send()
 
     def drain(s, _):
+        act_copy(s).wait()
         for kind in KINDS:
             for side in BOTH:
                 hop(s, wide, kind, side).wait_send()
@@ -387,7 +409,8 @@
             pltpu.SemaphoreType.DMA((TWO,)),
             pltpu.SemaphoreType.DMA((ty_size,)),
             pltpu.SemaphoreType.DMA((ty_size,)),
-            pltpu.SemaphoreType.DMA((len(KINDS),)),
+            pltpu.SemaphoreType.DMA((steps + 1,)),
+            pltpu.SemaphoreType.DMA((TWO,)),
         ],
         compiler_params=pltpu.CompilerParams(
             collective_id=0, has_side_effects=True, vmem_limit_bytes=56 * MIB
@@ -400,9 +423,9 @@
 
 def combine_kernel(
     ty_size,
-    q_in, k_in, v_in, act_in, x_in, wo, wd, lens,
+    q_in, kv_in, k_in, v_in, act_in, x_in, wo, wd, lens,
     y_out,
-    kc, vc, q_raw, q_f32, o_f32, att_out, att, mlp, wos, wds, yp, t1, xr, yf, p2_1, sd_1, sb_1, ra_1, rb_1, p2_2, sd_2, sb_2, ra_2, rb_2, ex,
+    kvn, kv_f32, kc, vc, q_raw, q_f32, o_f32, att_out, att, mlp, wos, wds, yp, t1, xr, yf, p2_1, sd_1, sb_1, ra_1, rb_1, p2_2, sd_2, sb_2, ra_2, rb_2, ex,
     qkv_sem, w_sem, wp_send, wp_recv, a2a_send, a2a_recv, mlp_sem, gx_send, gx_recv, x_sem, xp_send, xp_recv,
     rs_send, rs_recv, ag_send, ag_recv, out_sem, outp_send, outp_recv,
 ):
@@ -460,7 +483,7 @@
     x_swaps = [remote(x_tile(other, r), x_slot(core, r), xp_send.at[r], xp_recv.at[r], row_idx, tx_pair) for r in range(chunks)]
     qkv_loads = [
         pltpu.make_async_copy(src, dst, qkv_sem.at[n])
-        for n, (src, dst) in enumerate(((q_in, q_raw), (k_in, kc), (v_in, vc)))
+        for n, (src, dst) in enumerate(((q_in, q_raw), (kv_in, kvn), (k_in, kc), (v_in, vc)))
     ]
     for load in qkv_loads + w_loads + mlp_loads + x_loads:
         load.start()
@@ -508,18 +531,22 @@
             for h in range(heads):
                 lanes = slice(h * head_dim, (h + 1) * head_dim)
                 q_f32[h, k * seq_block : (k + 1) * seq_block, :] = q_raw[k, :, lanes].astype(F32)
+        kv_f32[...] = kvn[...].astype(F32)
         slots = lax.broadcasted_iota(jnp.int32, (heads * ty_size, kc.shape[1]), 1)
 
         def sequence(b, _):
             picked = pl.ds(b, ty_size, stride=seq_block)
+            fresh = pl.ds(core * seq_block + b, 1)
+            keys = updated(kc[b], kv_f32[0, fresh, :], lens[b])
+            vals = updated(vc[b], kv_f32[1, fresh, :], lens[b])
             queries = jnp.concatenate([q_f32[h, picked, :] for h in range(heads)]).astype(BF16)
             scores = lax.dot_general(
-                queries, kc[b], (((1,), (1,)), ((), ())), preferred_element_type=F32
+                queries, keys, (((1,), (1,)), ((), ())), preferred_element_type=F32
             ) * (head_dim**-0.5)
             scores = jnp.where(slots <= lens[b], scores, -1e30)
             weights = jnp.exp(scores - jnp.max(scores, axis=1, keepdims=True))
             probs = (weights / jnp.sum(weights, axis=1, keepdims=True)).astype(BF16)
-            mixed = jnp.dot(probs, vc[b], preferred_element_type=F32)
+            mixed = jnp.dot(probs, vals, preferred_element_type=F32)
             for h in range(heads):
                 o_f32[h, picked, :] = mixed[h * ty_size : (h + 1) * ty_size]
             return 0
@@ -782,9 +809,9 @@
         out_swap(r).wait()
 
 
-def combine(q_owned, k_out, v_out, lens_own, act_own, x_blk, w_out, w_down, ty_size):
+def combine(q_owned, kv_new, k_blk, v_blk, lens_own, act_own, x_blk, w_out, w_down, ty_size):
     seq_block = q_owned.shape[1]
-    head_dim = k_out.shape[TWO]
+    head_dim = k_blk.shape[TWO]
     chunks, most = len(SIZES), max(SIZES)
     group, half_ty = TWO * seq_block, ty_size // TWO
     cols = w_out.shape[1]
@@ -801,11 +828,13 @@
     y = pl.pallas_call(
         functools.partial(combine_kernel, ty_size),
         out_shape=jax.ShapeDtypeStruct(y_units, BF16),
-        in_specs=[any_spec] * 7 + [pl.BlockSpec(memory_space=pltpu.SMEM)],
+        in_specs=[any_spec] * 8 + [pl.BlockSpec(memory_space=pltpu.SMEM)],
         out_specs=any_spec,
         scratch_shapes=[
-            pltpu.VMEM(k_out.shape, BF16),
-            pltpu.VMEM(v_out.shape, BF16),
+            pltpu.VMEM(kv_new.shape, BF16),
+            pltpu.VMEM(kv_new.shape, F32),
+            pltpu.VMEM(k_blk.shape, BF16),
+            pltpu.VMEM(v_blk.shape, BF16),
             pltpu.VMEM(q_owned.shape, BF16),
             pltpu.VMEM((q_width // head_dim, ty_size * seq_block, head_dim), F32),
             pltpu.VMEM((q_width // head_dim, ty_size * seq_block, head_dim), F32),
@@ -820,7 +849,7 @@
             pltpu.VMEM(y_units, BF16),
             *ring_bufs,
             pltpu.VMEM((chunks, TWO, RING, most * group, cols), BF16),
-            dma((len(KINDS),)), dma((CORES,)), dma((CORES,)), dma((CORES,)),
+            dma((RING,)), dma((CORES,)), dma((CORES,)), dma((CORES,)),
             dma((ty_size,)), dma((half_ty, TWO)),
             dma((chunks,)),
             dma((chunks, TWO, TWO, TWO)), dma((chunks, TWO, TWO, TWO)),
@@ -833,8 +862,63 @@
             collective_id=1, has_side_effects=True, vmem_limit_bytes=60 * MIB
         ),
         name="combine",
-    )(q_owned, k_out, v_out, act_own.reshape(half_ty, group, ffn), x_blk.reshape(y_units), w_out, w_down, lens_own)
+    )(q_owned, kv_new, k_blk, v_blk, act_own.reshape(half_ty, group, ffn), x_blk.reshape(y_units), w_out, w_down, lens_own)
     return y.reshape(x_blk.shape)
+
+
+def emit_kernel(pieces, y_in, kv_in, k_in, v_in, lens, y_out, k_out, v_out, ys, kvn, kv_f32, kc, vc, load_sem, y_sem, out_sem, y_out_sem):
+    core = lax.axis_index("tx") % CORES
+    seq_block = kc.shape[0]
+    size = ys.shape[0] // pieces
+    loads = [
+        pltpu.make_async_copy(src, dst, load_sem.at[n]) for n, (src, dst) in enumerate(((kv_in, kvn), (k_in, kc), (v_in, vc)))
+    ]
+    part = [pl.ds(n * size, size) for n in range(pieces)]
+    y_loads = [pltpu.make_async_copy(y_in.at[p], ys.at[p], y_sem.at[n]) for n, p in enumerate(part)]
+    y_stores = [pltpu.make_async_copy(ys.at[p], y_out.at[p], y_out_sem.at[n]) for n, p in enumerate(part)]
+    stores = [pltpu.make_async_copy(kc, k_out, out_sem.at[0]), pltpu.make_async_copy(vc, v_out, out_sem.at[1])]
+    for load in loads + y_loads:
+        load.start()
+    for load in loads:
+        load.wait()
+    kv_f32[...] = kvn[...].astype(F32)
+
+    def sequence(b, _):
+        fresh = pl.ds(core * seq_block + b, 1)
+        kc[b] = updated(kc[b], kv_f32[0, fresh, :], lens[b])
+        vc[b] = updated(vc[b], kv_f32[1, fresh, :], lens[b])
+        return 0
+
+    lax.fori_loop(0, seq_block, sequence, 0, unroll=4)
+    for store in stores:
+        store.start()
+    for load, store in zip(y_loads, y_stores):
+        load.wait()
+        store.start()
+    for store in y_stores + stores:
+        store.wait()
+
+
+def emit(y, kv_new, k_blk, v_blk, lens_own):
+    pieces = 8
+    any_spec = pl.BlockSpec(memory_space=pl.ANY)
+    dma = pltpu.SemaphoreType.DMA
+    return pl.pallas_call(
+        functools.partial(emit_kernel, pieces),
+        out_shape=tuple(jax.ShapeDtypeStruct(a.shape, BF16) for a in (y, k_blk, v_blk)),
+        in_specs=[any_spec] * RING + [pl.BlockSpec(memory_space=pltpu.SMEM)],
+        out_specs=(any_spec,) * len(KINDS),
+        scratch_shapes=[
+            pltpu.VMEM(y.shape, BF16),
+            pltpu.VMEM(kv_new.shape, BF16),
+            pltpu.VMEM(kv_new.shape, F32),
+            pltpu.VMEM(k_blk.shape, BF16),
+            pltpu.VMEM(v_blk.shape, BF16),
+            dma((len(KINDS),)), dma((pieces,)), dma((TWO,)), dma((pieces,)),
+        ],
+        compiler_params=pltpu.CompilerParams(vmem_limit_bytes=60 * MIB),
+        name="emit",
+    )(y, kv_new, k_blk, v_blk, lens_own)
 
 
 def solution(mesh):
@@ -845,10 +929,9 @@
     def layer_shard(x_blk, lens_part, k_blk, v_blk, gamma_blk, w_query, w_key, w_value, w_gate, w_up, w_out, w_down):
         rows = x_blk.shape[0]
         d_model = x_blk.shape[1] * tx_size
-        seq_block, ctx_len, head_dim = k_blk.shape
+        seq_block, _, head_dim = k_blk.shape
         row_idx = lax.axis_index("ty")
         col_idx = lax.axis_index("tx")
-        ring_pos, core = col_idx // 2, col_idx % 2
         tile = min(256, w_gate.shape[1])
 
         block_start = (row_idx * tx_size + col_idx) * seq_block
@@ -857,13 +940,8 @@
             x_blk, gamma_blk, w_query, w_key, w_value, w_gate, w_up, lens_part, head_dim,
             ty_size, seq_block, d_model, tile,
         )
-        kv_own = lax.dynamic_slice_in_dim(kv_new, core * seq_block, seq_block, axis=1)
-        positions = jnp.arange(ctx_len)
-        at_slot = positions[None, :, None] == lens_own[:, None, None]
-        k_out = jnp.where(at_slot, kv_own[0][:, None, :], k_blk)
-        v_out = jnp.where(at_slot, kv_own[1][:, None, :], v_blk)
-
-        y_blk = combine(q_owned, k_out, v_out, lens_own, act_own, x_blk, w_out, w_down, ty_size)
+        y_raw = combine(q_owned, kv_new, k_blk, v_blk, lens_own, act_own, x_blk, w_out, w_down, ty_size)
+        y_blk, k_out, v_out = emit(y_raw, kv_new, k_blk, v_blk, lens_own)
         return y_blk, k_out, v_out
 
     in_specs = (P("dp", "tx"), P("dp"), cache_spec, cache_spec, P("tx"), P("tx", "ty"), P("tx", None), P("tx", None), P("tx", "ty"), P("tx", "ty"), P("ty", "tx"), P("ty", "tx"))

time: 225 us -> 223 us (level)
  Pallas kernels: 214 us -> 219 us
  local copies, waits for them, and re-layouts: 7.73 us -> 2.75 us
    pallas_call x0 -> x1, Pallas kernels: none -> 6.54 us  [emit(): pl.pallas_call(functools.partial(emit_kernel, pieces), out_shape=tuple((j...]
    unnamed x7 -> x0, local copies, waits for them, and re-layouts: 4.84 us -> none
where the time goes in v5:
time: 223 us
  Pallas kernels  219 us (98%)
  local copies, waits for them, and re-layouts  2.75 us (1%)
    pallas_call x1, Pallas kernels, project(): pl.pallas_call(functools.partial(project_kernel, ty_size, tile, d_model),...  112 us
    pallas_call x1, Pallas kernels, combine(): pl.pallas_call(functools.partial(combine_kernel, ty_size), out_shape=jax....  100 us
    pallas_call x1, Pallas kernels, emit(): pl.pallas_call(functools.partial(emit_kernel, pieces), out_shape=tuple((j...  6.54 us

profile of v5, /device:TPU:1, one launch (start us, length us, event | category | flops | bytes accessed | tf_op | source)
XLA Modules:
  0.0 222.8 jit_solution(12989526235087135794)
XLA Ops:
  0.6 1.4 dynamic_slice.3.lens
  2.0 1.4 reshape.30.lens
  3.4 112.3 %project.1 = (bf16[384,1536]{1,0:T(8,128)(2,1)}, bf16[16,24,384]{2,1,0:T(8,128)(2,1)}, bf16[2,48,128]{2,1,0:T(8,128)(2,1)}) custom-call(bf16[2,8,4,48,768]{4,3,2,1,0:T(8,128)(2,1)} %bitcast.6, bf16[16,4,48,768]{3,2,1,0:T(8,128)(2,1)} %bitcast.7, bf16[768,384]{1,0:T(8,128)(2,1)} %wq.1, bf16[768,128]{1,0:T(8,128)(2,1)} %wk.1, bf16[768,128]{1,0:T(8,128)(2,1)} %wv.1, ...), custom_call_target="tpu_custom_call" | custom-call | tf_op jit(solution)/shard_map/project/pallas_call | solution.py:373
  115.7 100.4 %combine.1 = bf16[2,64,24,768]{3,2,1,0:T(8,128)(2,1)} custom-call(bf16[16,24,384]{2,1,0:T(8,128)(2,1)} %get-tuple-element.6.q_in, bf16[2,48,128]{2,1,0:T(8,128)(2,1)} %get-tuple-element.7.kv_in, bf16[24,128,128]{2,1,0:T(8,128)(2,1)} %k_in.3, bf16[24,128,128]{2,1,0:T(8,128)(2,1)} %v_in.3, bf16[8,48,1536]{2,1,0:T(8,128)(2,1)} %bitcast.10, ...), custom_call_target="tpu_custom_call" | custom-call | tf_op jit(solution)/shard_map/combine/pallas_call | solution.py:828
  216.1 6.5 %emit.1 = (bf16[3072,768]{1,0:T(8,128)(2,1)}, bf16[24,128,128]{2,1,0:T(8,128)(2,1)}, bf16[24,128,128]{2,1,0:T(8,128)(2,1)}) custom-call(bf16[3072,768]{1,0:T(8,128)(2,1)} %bitcast.9, bf16[2,48,128]{2,1,0:T(8,128)(2,1)} %get-tuple-element.7.kv_in, bf16[24,128,128]{2,1,0:T(8,128)(2,1)} %k_in.3, bf16[24,128,128]{2,1,0:T(8,128)(2,1)} %v_in.3, s32[24]{0:T(128)} %dynamic_slice.3.lens), custom_call_target="tpu_custom_call" | custom-call | tf_op jit(solution)/shard_map/emit/pallas_call | solution.py:906

commit v6 on v5

--- a/solution.py
+++ b/solution.py
@@ -51,7 +51,7 @@
     ty_size, tile, d_model,
     x_main, x_kv, wq, wk, wv, wg, wu, gamma, lens, freqs,
     act_out, q_out, kv_out,
-    xs, ws, wkvs, gam, st, sr, p2, sd, sb, ra, rb, act, kvs, kvr, kvf, qs, qr,
+    spots, xs, ws, wkvs, gam, st, sr, p2, sd, sb, ra, rb, act, kvs, kvr, kvf, qs, qr,
     load_sem, pair_send, pair_recv, st_send, st_recv, ssem, rsem, kv_ssem, kv_rsem, kvf_sem, q_ssem, q_rsem, act_sem, out_sem,
 ):
     row_idx = lax.axis_index("ty")
@@ -223,8 +223,13 @@
 
     low = lax.broadcasted_iota(jnp.int32, (group, head_dim), 1) < head_dim // 2
 
-    def tables(positions):
-        angles = jnp.broadcast_to(positions.astype(F32), (head_dim, group)).T * freqs[...]
+    def tables(index, turns):
+        start = index * group
+        line = start // LANES
+        for n, at in enumerate((line, jnp.minimum(line + 1, lens.shape[0] - 1))):
+            down_rows = jnp.broadcast_to(lens[pl.ds(at, 1), :].astype(F32), (LANES, LANES)).T
+            spots[pl.ds(n * LANES, LANES), :] = down_rows
+        angles = spots[pl.ds(pl.multiple_of(start % LANES, 8), group), :] * (freqs[...] * turns)
         sines = jnp.sin(angles)
         return jnp.cos(angles), jnp.where(low, -sines, sines)
 
@@ -233,7 +238,7 @@
 
     def finish_q(half, vals):
         for g in range(hg):
-            cos2, sin2 = tables(lens[pl.ds((core * half_ty + half * hg + g) * RING + ring_pos, 1), :])
+            cos2, sin2 = tables((core * half_ty + half * hg + g) * RING + ring_pos, 1.0)
             for h in range(q_width // head_dim):
                 cols = slice(h * head_dim, (h + 1) * head_dim)
                 turned = turn(vals[g * group : (g + 1) * group, cols], cos2, sin2).astype(BF16)
@@ -293,7 +298,7 @@
     for n, pos in enumerate((pos_p, pos_m, pos_o)):
         kv_copy(n, pos).wait_recv()
     new_row = (kvs[ring_pos] + kvr[0]) + (kvr[1] + kvr[2])
-    kvf[core] = turn(new_row, *tables(lens[pl.ds(row_idx * RING + ring_pos, 1), :] * other)).astype(BF16)
+    kvf[core] = turn(new_row, *tables(row_idx * RING + ring_pos, other.astype(F32))).astype(BF16)
     kv_pair = remote(kvf.at[core], kvf.at[core], kvf_sem.at[0], kvf_sem.at[1], row_idx, tx_pair)
     kv_pair.start()
     weights_here(2, 2)
@@ -380,6 +385,7 @@
         in_specs=[any_spec] * 8 + [vmem_spec] * 2,
         out_specs=(any_spec,) * 3,
         scratch_shapes=[
+            pltpu.VMEM((TWO * LANES, LANES), F32),
             pltpu.VMEM((RING * half_ty + RING, group, kdim), BF16),
             pltpu.VMEM((steps + 1, kdim, wide), BF16),
             pltpu.VMEM((kdim, kv_width), BF16),
@@ -417,7 +423,7 @@
         ),
         name="project",
     )(
-        x_main, x_kv, wq, wk, wv, wg, wu, gamma_blk.reshape(-1, LANES), lens.reshape(-1, group), inverse_freqs(head_dim)
+        x_main, x_kv, wq, wk, wv, wg, wu, gamma_blk.reshape(-1, LANES), lens.reshape(-1, LANES), inverse_freqs(head_dim)
     )
 
 
@@ -537,13 +543,14 @@
         def sequence(b, _):
             picked = pl.ds(b, ty_size, stride=seq_block)
             fresh = pl.ds(core * seq_block + b, 1)
-            keys = updated(kc[b], kv_f32[0, fresh, :], lens[b])
-            vals = updated(vc[b], kv_f32[1, fresh, :], lens[b])
+            length = lens[(row_idx * TWO * RING + col_idx) * seq_block + b]
+            keys = updated(kc[b], kv_f32[0, fresh, :], length)
+            vals = updated(vc[b], kv_f32[1, fresh, :], length)
             queries = jnp.concatenate([q_f32[h, picked, :] for h in range(heads)]).astype(BF16)
             scores = lax.dot_general(
                 queries, keys, (((1,), (1,)), ((), ())), preferred_element_type=F32
             ) * (head_dim**-0.5)
-            scores = jnp.where(slots <= lens[b], scores, -1e30)
+            scores = jnp.where(slots <= length, scores, -1e30)
             weights = jnp.exp(scores - jnp.max(scores, axis=1, keepdims=True))
             probs = (weights / jnp.sum(weights, axis=1, keepdims=True)).astype(BF16)
             mixed = jnp.dot(probs, vals, preferred_element_type=F32)
@@ -870,6 +877,7 @@
     core = lax.axis_index("tx") % CORES
     seq_block = kc.shape[0]
     size = ys.shape[0] // pieces
+    base = (lax.axis_index("ty") * TWO * RING + lax.axis_index("tx")) * seq_block
     loads = [
         pltpu.make_async_copy(src, dst, load_sem.at[n]) for n, (src, dst) in enumerate(((kv_in, kvn), (k_in, kc), (v_in, vc)))
     ]
@@ -877,23 +885,24 @@
     y_loads = [pltpu.make_async_copy(y_in.at[p], ys.at[p], y_sem.at[n]) for n, p in enumerate(part)]
     y_stores = [pltpu.make_async_copy(ys.at[p], y_out.at[p], y_out_sem.at[n]) for n, p in enumerate(part)]
     stores = [pltpu.make_async_copy(kc, k_out, out_sem.at[0]), pltpu.make_async_copy(vc, v_out, out_sem.at[1])]
-    for load in loads + y_loads:
+    for load in y_loads + loads:
         load.start()
+    for load, store in zip(y_loads, y_stores):
+        load.wait()
+        store.start()
     for load in loads:
         load.wait()
     kv_f32[...] = kvn[...].astype(F32)
 
     def sequence(b, _):
         fresh = pl.ds(core * seq_block + b, 1)
-        kc[b] = updated(kc[b], kv_f32[0, fresh, :], lens[b])
-        vc[b] = updated(vc[b], kv_f32[1, fresh, :], lens[b])
+        length = lens[base + b]
+        kc[b] = updated(kc[b], kv_f32[0, fresh, :], length)
+        vc[b] = updated(vc[b], kv_f32[1, fresh, :], length)
         return 0
 
     lax.fori_loop(0, seq_block, sequence, 0, unroll=4)
     for store in stores:
-        store.start()
-    for load, store in zip(y_loads, y_stores):
-        load.wait()
         store.start()
     for store in y_stores + stores:
         store.wait()
@@ -930,18 +939,14 @@
         rows = x_blk.shape[0]
         d_model = x_blk.shape[1] * tx_size
         seq_block, _, head_dim = k_blk.shape
-        row_idx = lax.axis_index("ty")
-        col_idx = lax.axis_index("tx")
         tile = min(256, w_gate.shape[1])
 
-        block_start = (row_idx * tx_size + col_idx) * seq_block
-        lens_own = lax.dynamic_slice_in_dim(lens_part, block_start, seq_block)
         act_own, q_owned, kv_new = project(
             x_blk, gamma_blk, w_query, w_key, w_value, w_gate, w_up, lens_part, head_dim,
             ty_size, seq_block, d_model, tile,
         )
-        y_raw = combine(q_owned, kv_new, k_blk, v_blk, lens_own, act_own, x_blk, w_out, w_down, ty_size)
-        y_blk, k_out, v_out = emit(y_raw, kv_new, k_blk, v_blk, lens_own)
+        y_raw = combine(q_owned, kv_new, k_blk, v_blk, lens_part, act_own, x_blk, w_out, w_down, ty_size)
+        y_blk, k_out, v_out = emit(y_raw, kv_new, k_blk, v_blk, lens_part)
         return y_blk, k_out, v_out
 
     in_specs = (P("dp", "tx"), P("dp"), cache_spec, cache_spec, P("tx"), P("tx", "ty"), P("tx", None), P("tx", None), P("tx", "ty"), P("tx", "ty"), P("ty", "tx"), P("ty", "tx"))

time: 223 us -> 221 us (level)
  local copies, waits for them, and re-layouts: 2.75 us -> 0 us
where the time goes in v6:
time: 221 us
  Pallas kernels  220 us (100%)
    pallas_call x1, Pallas kernels, project(): pl.pallas_call(functools.partial(project_kernel, ty_size, tile, d_model),...  112 us
    pallas_call x1, Pallas kernels, combine(): pl.pallas_call(functools.partial(combine_kernel, ty_size), out_shape=jax....  101 us
    pallas_call x1, Pallas kernels, emit(): pl.pallas_call(functools.partial(emit_kernel, pieces), out_shape=tuple((j...  6.83 us

profile of v6, /device:TPU:1, one launch (start us, length us, event | category | flops | bytes accessed | tf_op | source)
XLA Modules:
  0.0 220.5 jit_solution(7520630455024682479)
XLA Ops:
  0.6 112.2 %project.1 = (bf16[384,1536]{1,0:T(8,128)(2,1)}, bf16[16,24,384]{2,1,0:T(8,128)(2,1)}, bf16[2,48,128]{2,1,0:T(8,128)(2,1)}) custom-call(bf16[2,8,4,48,768]{4,3,2,1,0:T(8,128)(2,1)} %bitcast.7, bf16[16,4,48,768]{3,2,1,0:T(8,128)(2,1)} %bitcast.8, bf16[768,384]{1,0:T(8,128)(2,1)} %wq.1, bf16[768,128]{1,0:T(8,128)(2,1)} %wk.1, bf16[768,128]{1,0:T(8,128)(2,1)} %wv.1, ...), custom_call_target="tpu_custom_call" | custom-call | tf_op jit(solution)/shard_map/project/pallas_call | solution.py:378
  112.9 100.6 %combine.1 = bf16[2,64,24,768]{3,2,1,0:T(8,128)(2,1)} custom-call(bf16[16,24,384]{2,1,0:T(8,128)(2,1)} %get-tuple-element.6.q_in, bf16[2,48,128]{2,1,0:T(8,128)(2,1)} %get-tuple-element.7.kv_in, bf16[24,128,128]{2,1,0:T(8,128)(2,1)} %k_in.3, bf16[24,128,128]{2,1,0:T(8,128)(2,1)} %v_in.3, bf16[8,48,1536]{2,1,0:T(8,128)(2,1)} %bitcast.11, ...), custom_call_target="tpu_custom_call" | custom-call | tf_op jit(solution)/shard_map/combine/pallas_call | solution.py:835
  213.5 6.8 %emit.1 = (bf16[3072,768]{1,0:T(8,128)(2,1)}, bf16[24,128,128]{2,1,0:T(8,128)(2,1)}, bf16[24,128,128]{2,1,0:T(8,128)(2,1)}) custom-call(bf16[3072,768]{1,0:T(8,128)(2,1)} %bitcast.10, bf16[2,48,128]{2,1,0:T(8,128)(2,1)} %get-tuple-element.7.kv_in, bf16[24,128,128]{2,1,0:T(8,128)(2,1)} %k_in.3, bf16[24,128,128]{2,1,0:T(8,128)(2,1)} %v_in.3, s32[3072]{0:T(1024)} %lens.3), custom_call_target="tpu_custom_call" | custom-call | tf_op jit(solution)/shard_map/emit/pallas_call | solution.py:915

commit v7 on v6

--- a/solution.py
+++ b/solution.py
@@ -19,11 +19,11 @@
 BOTH = (0, 1)
 KINDS = (0, 1, 2)
 MIB = 2**20
-SIZES = (1, 2, 2, 2, 1)
+SIZES = (2, 2, 2, 1, 1)
 ORDER = (
-    "m1A0m0g1a0a1g0h0a2h1m2h2m3202130g2314041a3a451g35022h3616032"
-    + "m42371g4h4423381522443903462539144637254738283649293t194t0t3"
-    + "t2t4"
+    "m2m1A0a0a1g1h1a2m021h2g2h031g0m4a4m3412251a320g4h43230h3g361"
+    + "2442407123345250816044336270915472438053t182636490929394t2t0"
+    + "t3t4"
 )
 F32 = jnp.float32
 BF16 = jnp.bfloat16

time: 221 us -> 219 us (level)
  no operation moved by 1% of the time
where the time goes in v7:
time: 219 us
  Pallas kernels  218 us (100%)
    pallas_call x1, Pallas kernels, project(): pl.pallas_call(functools.partial(project_kernel, ty_size, tile, d_model),...  112 us
    pallas_call x1, Pallas kernels, combine(): pl.pallas_call(functools.partial(combine_kernel, ty_size), out_shape=jax....  99.2 us
    pallas_call x1, Pallas kernels, emit(): pl.pallas_call(functools.partial(emit_kernel, pieces), out_shape=tuple((j...  6.83 us

profile of v7, /device:TPU:1, one launch (start us, length us, event | category | flops | bytes accessed | tf_op | source)
XLA Modules:
  0.0 219.1 jit_solution(5461539714242577196)
XLA Ops:
  0.6 112.2 %project.1 = (bf16[384,1536]{1,0:T(8,128)(2,1)}, bf16[16,24,384]{2,1,0:T(8,128)(2,1)}, bf16[2,48,128]{2,1,0:T(8,128)(2,1)}) custom-call(bf16[2,8,4,48,768]{4,3,2,1,0:T(8,128)(2,1)} %bitcast.7, bf16[16,4,48,768]{3,2,1,0:T(8,128)(2,1)} %bitcast.8, bf16[768,384]{1,0:T(8,128)(2,1)} %wq.1, bf16[768,128]{1,0:T(8,128)(2,1)} %wk.1, bf16[768,128]{1,0:T(8,128)(2,1)} %wv.1, ...), custom_call_target="tpu_custom_call" | custom-call | tf_op jit(solution)/shard_map/project/pallas_call | solution.py:378
  112.9 99.2 %combine.1 = bf16[2,64,24,768]{3,2,1,0:T(8,128)(2,1)} custom-call(bf16[16,24,384]{2,1,0:T(8,128)(2,1)} %get-tuple-element.6.q_in, bf16[2,48,128]{2,1,0:T(8,128)(2,1)} %get-tuple-element.7.kv_in, bf16[24,128,128]{2,1,0:T(8,128)(2,1)} %k_in.3, bf16[24,128,128]{2,1,0:T(8,128)(2,1)} %v_in.3, bf16[8,48,1536]{2,1,0:T(8,128)(2,1)} %bitcast.11, ...), custom_call_target="tpu_custom_call" | custom-call | tf_op jit(solution)/shard_map/combine/pallas_call | solution.py:835
  212.1 6.8 %emit.1 = (bf16[3072,768]{1,0:T(8,128)(2,1)}, bf16[24,128,128]{2,1,0:T(8,128)(2,1)}, bf16[24,128,128]{2,1,0:T(8,128)(2,1)}) custom-call(bf16[3072,768]{1,0:T(8,128)(2,1)} %bitcast.10, bf16[2,48,128]{2,1,0:T(8,128)(2,1)} %get-tuple-element.7.kv_in, bf16[24,128,128]{2,1,0:T(8,128)(2,1)} %k_in.3, bf16[24,128,128]{2,1,0:T(8,128)(2,1)} %v_in.3, s32[3072]{0:T(1024)} %lens.3), custom_call_target="tpu_custom_call" | custom-call | tf_op jit(solution)/shard_map/emit/pallas_call | solution.py:915
